TPU v7x, 8 devices: a whole 2x2x1 slice. The times are simulated.
8 devices in a mesh: dp: 2 (over z, y), tp: 4 (over x, core).
Axes of the slice: x: 2, y: 2, z: 1, core: 2. Of those that a mesh axis runs over, the one named last changes fastest.
Arguments:
- hidden: bfloat16 [512, 2048], P('dp'), parts along dimension 0
- positions: int32 [512], P('dp'), parts along dimension 0
- k_cache: bfloat16 [2, 512, 64, 8, 128], P(None, 'dp', None, 'tp'), parts along dimension 1
- v_cache: bfloat16 [2, 512, 64, 8, 128], P(None, 'dp', None, 'tp'), parts along dimension 1
- attn_norm: bfloat16 [2, 2048], replicated
- w_query: bfloat16 [2, 2048, 2048], P(None, None, 'tp')
- w_key: bfloat16 [2, 2048, 1024], P(None, None, 'tp')
- w_value: bfloat16 [2, 2048, 1024], P(None, None, 'tp')
- w_out: bfloat16 [2, 2048, 2048], P(None, 'tp')
- mlp_norm: bfloat16 [2, 2048], replicated
- w_gate: bfloat16 [2, 2048, 8192], P(None, None, 'tp')
- w_up: bfloat16 [2, 2048, 8192], P(None, None, 'tp')
- w_down: bfloat16 [2, 8192, 2048], P(None, 'tp')
Outputs:
- output 1: bfloat16 [512, 2048], P('dp'), parts along dimension 0
- output 2: bfloat16 [2, 512, 64, 8, 128], P(None, 'dp', None, 'tp'), parts along dimension 1
- output 3: bfloat16 [2, 512, 64, 8, 128], P(None, 'dp', None, 'tp'), parts along dimension 1
There are 2 independent parts. A program takes and returns all parts, laid end to end along the dimension named above; an argument that names none is the same for every part.
All inputs are finite; a program needn't handle non-finite values.
Results may differ from a plain program's by a relative error of at most 0.02.
Values are sent between devices in bfloat16 or wider.
A program may use at most 1 GiB of HBM per device.

v0:
```python
import math
import jax
import jax.numpy as jnp
from jax import lax
from jax.sharding import PartitionSpec as P


def rms_norm(hidden, weight):
    hidden_f32 = hidden.astype(jnp.float32)
    mean_sq = jnp.mean(hidden_f32 * hidden_f32, axis=-1, keepdims=True)
    return (hidden_f32 * lax.rsqrt(mean_sq + 1e-5) * weight.astype(jnp.float32)).astype(jnp.bfloat16)


def rope_tables(positions, head_dim):
    half_dim = head_dim // 2
    inv_freq = jnp.power(500000.0, -jnp.arange(half_dim, dtype=jnp.float32) * (2.0 / head_dim))
    wavelen = (2.0 * math.pi) / inv_freq
    smooth = (8192.0 / wavelen - 1.0) / 3.0
    blended = (1.0 - smooth) * inv_freq / 8.0 + smooth * inv_freq
    scaled = jnp.where(wavelen < 2048.0, inv_freq, jnp.where(wavelen > 8192.0, inv_freq / 8.0, blended))
    angles = positions.astype(jnp.float32)[:, None] * scaled[None, :]
    return jnp.cos(angles), jnp.sin(angles)


def apply_rope(vectors, cos_tab, sin_tab):
    half_dim = vectors.shape[-1] // 2
    vec_f32 = vectors.astype(jnp.float32)
    first = vec_f32[..., :half_dim]
    second = vec_f32[..., half_dim:]
    cos_b = cos_tab[:, None, :]
    sin_b = sin_tab[:, None, :]
    return jnp.concatenate([first * cos_b - second * sin_b, second * cos_b + first * sin_b], axis=-1).astype(jnp.bfloat16)


def attend_split(query, k_old, v_old, key_new, value_new, before):
    score_scale = query.shape[-1] ** -0.5
    scores = jnp.einsum('bkgd,bskd->bkgs', query, k_old, preferred_element_type=jnp.float32) * score_scale
    scores = jnp.where(before, scores, -jnp.inf)
    score_new = jnp.einsum('clhe,cle->clh', query, key_new, preferred_element_type=jnp.float32) * score_scale
    row_peak = jnp.maximum(jnp.max(scores, axis=-1), score_new)
    weight_old = jnp.exp(scores - row_peak[..., None])
    weight_new = jnp.exp(score_new - row_peak)
    inv_total = 1.0 / (jnp.sum(weight_old, axis=-1) + weight_new)
    prob_old = (weight_old * inv_total[..., None]).astype(jnp.bfloat16)
    prob_new = (weight_new * inv_total).astype(jnp.bfloat16)
    attn_out = jnp.einsum('bkgs,bskd->bkgd', prob_old, v_old, preferred_element_type=jnp.float32)
    attn_out = attn_out + prob_new[..., None].astype(jnp.float32) * value_new[:, :, None, :].astype(jnp.float32)
    return attn_out.astype(jnp.bfloat16)


def attention_block(hidden, norm_weight, wq_layer, wk_layer, wv_layer, wo_layer, k_old, v_old, cos_tab, sin_tab, before):
    batch_size = hidden.shape[0]
    kv_heads = k_old.shape[2]
    head_dim = k_old.shape[3]
    q_heads = wq_layer.shape[1] // head_dim
    normed = rms_norm(hidden, norm_weight)
    query = jnp.dot(normed, wq_layer, preferred_element_type=jnp.float32).astype(jnp.bfloat16)
    key_new = jnp.dot(normed, wk_layer, preferred_element_type=jnp.float32).astype(jnp.bfloat16)
    value_new = jnp.dot(normed, wv_layer, preferred_element_type=jnp.float32).astype(jnp.bfloat16)
    query = apply_rope(query.reshape(batch_size, q_heads, head_dim), cos_tab, sin_tab)
    key_new = apply_rope(key_new.reshape(batch_size, kv_heads, head_dim), cos_tab, sin_tab)
    value_new = value_new.reshape(batch_size, kv_heads, head_dim)
    attended = attend_split(query.reshape(batch_size, kv_heads, q_heads // kv_heads, head_dim), k_old, v_old, key_new, value_new, before)
    mixed = jnp.dot(attended.reshape(batch_size, q_heads * head_dim), wo_layer, preferred_element_type=jnp.float32)
    return mixed.astype(jnp.bfloat16), key_new, value_new


def mlp_block(hidden, norm_weight, wg_layer, wu_layer, wd_layer):
    normed = rms_norm(hidden, norm_weight)
    gate_proj = jnp.dot(normed, wg_layer, preferred_element_type=jnp.float32).astype(jnp.bfloat16)
    up_proj = jnp.dot(normed, wu_layer, preferred_element_type=jnp.float32).astype(jnp.bfloat16)
    activated = (jax.nn.silu(gate_proj.astype(jnp.float32)) * up_proj.astype(jnp.float32)).astype(jnp.bfloat16)
    return jnp.dot(activated, wd_layer, preferred_element_type=jnp.float32).astype(jnp.bfloat16)


def write_rows(cache, rows, positions):
    at_pos = (jnp.arange(cache.shape[2])[None, :] == positions[:, None])[None, :, :, None, None]
    return jnp.where(at_pos, rows[:, :, None], cache)


def solution(mesh):
    row_spec = P('dp', None)
    pos_spec = P('dp')
    cache_spec = P(None, 'dp', None, 'tp', None)
    norm_spec = P(None, None)
    col_spec = P(None, None, 'tp')
    split_rows = P(None, 'tp', None)

    def local_step(hidden, positions, k_cache, v_cache, attn_norm, w_query, w_key, w_value, w_out, mlp_norm, w_gate, w_up, w_down):
        cos_tab, sin_tab = rope_tables(positions, k_cache.shape[4])
        before = (jnp.arange(k_cache.shape[2])[None, :] < positions[:, None])[:, None, None, :]
        k_rows = []
        v_rows = []
        for layer in range(k_cache.shape[0]):
            part_out, key_new, value_new = attention_block(hidden, attn_norm[layer], w_query[layer], w_key[layer], w_value[layer], w_out[layer], k_cache[layer], v_cache[layer], cos_tab, sin_tab, before)
            hidden = hidden + lax.psum(part_out, 'tp')
            part_out = mlp_block(hidden, mlp_norm[layer], w_gate[layer], w_up[layer], w_down[layer])
            hidden = hidden + lax.psum(part_out, 'tp')
            k_rows.append(key_new)
            v_rows.append(value_new)
        k_out = write_rows(k_cache, jnp.stack(k_rows), positions)
        v_out = write_rows(v_cache, jnp.stack(v_rows), positions)
        return hidden, k_out, v_out

    return jax.shard_map(local_step, mesh=mesh, in_specs=(row_spec, pos_spec, cache_spec, cache_spec, norm_spec, col_spec, col_spec, col_spec, split_rows, norm_spec, col_spec, col_spec, split_rows), out_specs=(row_spec, cache_spec, cache_spec), check_vma=False)
```

profile of v0, /device:TPU:0, one launch (start us, length us, event | category | flops | bytes accessed | tf_op | source)
XLA Modules:
  0.0 293.4 jit_solution(11851838401572195385)
XLA Ops:
  7.9 1.4 iota_compare_fusion
  9.3 1.5 fusion.58
  10.9 0.8 slice_convert_fusion.1
  12.2 2.4 convolution_convert_fusion.4
  16.0 2.3 fusion.95
  19.0 1.5 multiply_reduce_fusion.1
  20.6 16.5 %fusion.140 = (bf16[1,256,64,2,128]{4,3,2,1,0:T(2,128)(2,1)}, bf16[1,256,64,2,128]{4,3,2,1,0:T(2,128)(2,1)S(1)}) fusion(bf16[2,256,64,2,128]{4,3,2,1,0:T(2,128)(2,1)} %param.15), kind=kLoop, calls=%fused_computation.158 | loop fusion | bytes 33554432 | tf_op jit(solution)/shard_map/slice | solution.py:95
  37.2 5.2 %fusion.142 = (f32[256,2,2]{2,1,0:T(2,128)S(1)}, f32[256,2,2,64]{3,2,1,0:T(2,128)S(1)}) fusion(bf16[1,256,64,2,128]{4,3,2,1,0:T(2,128)(2,1)S(1)} %get-tuple-element.14, bf16[256,2,2,64]{3,2,1,0:T(2,128)(2,1)S(1)} %bitcast.141, bf16[256,2,2,64]{3,2,1,0:T(2,128)(2,1)S(1)} %bitcast.139, pred[256,64]{1,0:T(8,128)(4,1)S(1)} %copy-done.9), kind=kOutput, calls=%fused_computation.160 | convolution fusion | flops 17497088 | bytes 8933376 | tf_op jit(solution)/shard_map/bkgd,bskd->bkgs/dot_general | solution.py:37
  42.7 1.4 fusion.124
  44.6 16.2 %fusion.141 = (bf16[1,256,64,2,128]{4,3,2,1,0:T(2,128)(2,1)}, bf16[1,256,64,2,128]{4,3,2,1,0:T(2,128)(2,1)S(1)}) fusion(bf16[2,256,64,2,128]{4,3,2,1,0:T(2,128)(2,1)} %param.16), kind=kLoop, calls=%fused_computation.159 | loop fusion | bytes 33554432 | tf_op jit(solution)/shard_map/slice | solution.py:95
  60.9 3.0 %fusion.100 = bf16[256,2,2,128]{3,2,1,0:T(2,128)(2,1)S(1)} fusion(bf16[1,256,64,2,128]{4,3,2,1,0:T(2,128)(2,1)S(1)} %get-tuple-element.16, f32[256,2,2,64]{3,2,1,0:T(2,128)S(1)} %get-tuple-element.36, f32[256,2,128]{2,1,0:T(2,128)S(1)} %copy.51, f32[256,2,2]{2,1,0:T(2,128)S(1)} %copy.50, f32[256,2,2]{2,1,0:T(2,128)S(1)} %copy.48, f32[256,2,2]{2,1,0:T(2,128)S(1)} %copy.46), kind=kOutput, calls=%fused_computation.88 | convolution fusion | flops 17367040 | bytes 9187328 | tf_op jit(solution)/shard_map/bkgs,bskd->bkgd/dot_general | solution.py:46
  64.0 3.3 %convolution_convert_fusion.1 = bf16[256,2048]{1,0:T(8,128)(2,1)} fusion(bf16[256,512]{1,0:T(8,128)(2,1)S(1)} %reshape.259, bf16[2,512,2048]{2,1,0:T(8,128)(2,1)} %param.21), kind=kOutput, calls=%fused_computation.41 | convolution fusion | flops 537395200 | bytes 3407872 | tf_op jit(solution)/shard_map/dot_general | solution.py:64
  67.9 33.2 %all-reduce.5.cloned.1.call-done = bf16[256,2048]{1,0:T(8,128)(2,1)} async-done(((bf16[256,2048]{1,0:T(8,128)(2,1)}), bf16[256,2048]{1,0:T(8,128)(2,1)}) %all-reduce.5.cloned.1.call-update) | async-done | bytes 1048592 | tf_op jit(solution)/shard_map/psum | solution.py:96
  101.1 1.7 fusion.61
  102.9 5.8 %fusion.22 = bf16[256,2048]{1,0:T(8,128)(2,1)S(1)} fusion(bf16[2,2048,2048]{2,1,0:T(8,128)(2,1)} %param.23, bf16[256,2048]{1,0:T(8,128)(2,1)S(1)} %get-tuple-element.10, f32[2048]{0:T(1024)S(1)} %bitcast.164, f32[256]{0:T(256)S(1)} %add_rsqrt_fusion.2), kind=kOutput, calls=%fused_computation.42 | convolution fusion | flops 2150105088 | bytes 10494976 | tf_op jit(solution)/shard_map/dot_general | solution.py:70
  108.7 11.4 %fusion.37 = bf16[256,2048]{1,0:T(8,128)(2,1)} fusion(bf16[2,2048,2048]{2,1,0:T(8,128)(2,1)} %param.25, bf16[2,2048,2048]{2,1,0:T(8,128)(2,1)} %param.24, bf16[256,2048]{1,0:T(8,128)(2,1)S(1)} %fusion.22, bf16[256,2048]{1,0:T(8,128)(2,1)S(1)} %get-tuple-element.10, f32[2048]{0:T(1024)S(1)} %bitcast.165, f32[256]{0:T(256)S(1)} %add_rsqrt_fusion.2), kind=kOutput, calls=%fused_computation.47 | convolution fusion | flops 4302307328 | bytes 19932160 | tf_op jit(solution)/shard_map/dot_general | solution.py:73
  120.4 31.0 %all-reduce.7.cloned.1.call-done = bf16[256,2048]{1,0:T(8,128)(2,1)} async-done(((bf16[256,2048]{1,0:T(8,128)(2,1)}), bf16[256,2048]{1,0:T(8,128)(2,1)}) %all-reduce.7.cloned.1.call-update) | async-done | bytes 1048592 | tf_op jit(solution)/shard_map/psum | solution.py:98
  151.4 1.7 fusion.67
  153.1 2.0 convolution_convert_fusion.2
  156.2 0.8 fusion.92
  157.3 0.8 copy.59
  158.8 8.3 %fusion.143 = (f32[256,2,2]{2,1,0:T(2,128)S(1)}, f32[256,2,2,64]{3,2,1,0:T(2,128)S(1)}) fusion(bf16[1,256,64,2,128]{4,3,2,1,0:T(2,128)(2,1)} %get-tuple-element.13, bf16[256,2,2,64]{3,2,1,0:T(2,128)(2,1)S(1)} %bitcast.144, bf16[256,2,2,64]{3,2,1,0:T(2,128)(2,1)S(1)} %bitcast.142, pred[256,64]{1,0:T(8,128)(4,1)S(1)} %copy-done.10), kind=kOutput, calls=%fused_computation.161 | convolution fusion | flops 17497088 | bytes 8933376 | tf_op jit(solution)/shard_map/bkgd,bskd->bkgs/dot_general | solution.py:37
  167.1 1.5 multiply_reduce_fusion
  169.0 1.6 fusion.125
  171.2 6.2 %fusion.103 = bf16[256,2,2,128]{3,2,1,0:T(2,128)(2,1)S(1)} fusion(bf16[1,256,64,2,128]{4,3,2,1,0:T(2,128)(2,1)} %get-tuple-element.15, f32[256,2,2,64]{3,2,1,0:T(2,128)S(1)} %get-tuple-element.38, f32[256,2,128]{2,1,0:T(2,128)S(1)} %copy-done.7, f32[256,2,2]{2,1,0:T(2,128)S(1)} %copy.58, f32[256,2,2]{2,1,0:T(2,128)S(1)} %copy.56, f32[256,2,2]{2,1,0:T(2,128)S(1)} %copy.54), kind=kOutput, calls=%fused_computation.91 | convolution fusion | flops 17367040 | bytes 9187328 | tf_op jit(solution)/shard_map/bkgs,bskd->bkgd/dot_general | solution.py:46
  177.6 3.3 %convolution_convert_fusion = bf16[256,2048]{1,0:T(8,128)(2,1)} fusion(bf16[256,512]{1,0:T(8,128)(2,1)S(1)} %reshape.260, bf16[2,512,2048]{2,1,0:T(8,128)(2,1)} %param.21), kind=kOutput, calls=%fused_computation.40 | convolution fusion | flops 537395200 | bytes 3407872 | tf_op jit(solution)/shard_map/dot_general | solution.py:64
  181.4 30.8 %all-reduce.9.cloned.1.call-done = bf16[256,2048]{1,0:T(8,128)(2,1)} async-done(((bf16[256,2048]{1,0:T(8,128)(2,1)}), bf16[256,2048]{1,0:T(8,128)(2,1)}) %all-reduce.9.cloned.1.call-update) | async-done | bytes 1048592 | tf_op jit(solution)/shard_map/psum | solution.py:96
  212.2 1.7 fusion.70
  214.0 6.7 %fusion.40 = bf16[256,2048]{1,0:T(8,128)(2,1)} fusion(bf16[2,2048,2048]{2,1,0:T(8,128)(2,1)} %param.23, bf16[256,2048]{1,0:T(8,128)(2,1)S(1)} %get-tuple-element.4, f32[2048]{0:T(1024)S(1)} %bitcast.156, f32[256]{0:T(256)S(1)} %add_rsqrt_fusion), kind=kOutput, calls=%fused_computation.48 | convolution fusion | flops 2150105088 | bytes 10494976 | tf_op jit(solution)/shard_map/dot_general | solution.py:70
  220.7 11.8 %fusion.55 = bf16[256,2048]{1,0:T(8,128)(2,1)} fusion(bf16[2,2048,2048]{2,1,0:T(8,128)(2,1)} %param.25, bf16[2,2048,2048]{2,1,0:T(8,128)(2,1)} %param.24, bf16[256,2048]{1,0:T(8,128)(2,1)} %fusion.40, bf16[256,2048]{1,0:T(8,128)(2,1)S(1)} %get-tuple-element.4, f32[2048]{0:T(1024)S(1)} %bitcast.157, f32[256]{0:T(256)S(1)} %add_rsqrt_fusion), kind=kOutput, calls=%fused_computation.53 | convolution fusion | flops 4302307328 | bytes 19932160 | tf_op jit(solution)/shard_map/dot_general | solution.py:73
  232.5 51.5 %broadcast_select_fusion = (bf16[2,256,64,2,128]{4,3,2,1,0:T(2,128)(2,1)}, bf16[2,256,64,2,128]{4,3,2,1,0:T(2,128)(2,1)}) fusion(bf16[2,256,64,2,128]{4,3,2,1,0:T(2,128)(2,1)} %param.16, pred[256,64]{1,0:T(8,128)(4,1)S(1)} %copy-done.8, bf16[2,256,2,128]{3,2,1,0:T(2,128)(2,1)S(1)} %copy.61, bf16[2,256,64,2,128]{4,3,2,1,0:T(2,128)(2,1)} %param.15, ...), kind=kLoop, calls=%fused_computation | loop fusion | flops 16777216 | bytes 67649536 | tf_op jit(solution)/shard_map/jit(_where)/select_n | solution.py:78
  284.1 2.6 add.113
  (86 shorter events, 8.6 us)
Async XLA Ops:
  7.2 94.0 %all-reduce.5.cloned.1.call-start = ((), (), s32[]{:S(2)}) async-start(), calls=%async_computation | async-start | bytes 2097152 | tf_op jit(solution)/shard_map/psum | solution.py:96
  10.8 3.7 %copy-start = (bf16[256,2048]{1,0:T(8,128)(2,1)S(1)}, bf16[256,2048]{1,0:T(8,128)(2,1)}, u32[]{:S(2)}) copy-start(bf16[256,2048]{1,0:T(8,128)(2,1)} %param.13) | copy-start | bytes 3145732
  12.2 2.4 copy-start.13
  14.6 1.0 copy-start.5
  15.3 0.6 copy-start.1
  15.4 0.6 copy-start.3
  20.6 16.5 %copy-start.9 = (pred[256,64]{1,0:T(8,128)(4,1)S(1)}, pred[256,64]{1,0:T(8,128)(4,1)}, u32[]{:S(2)}) copy-start(pred[256,64]{1,0:T(8,128)(4,1)} %get-tuple-element.34) | copy-start | bytes 49156
  64.0 3.9 %copy-start.11 = (bf16[2,2048]{1,0:T(2,128)(2,1)S(1)}, bf16[2,2048]{1,0:T(2,128)(2,1)}, u32[]{:S(2)}) copy-start(bf16[2,2048]{1,0:T(2,128)(2,1)} %param.22) | copy-start | bytes 24580
  67.3 84.1 %all-reduce.7.cloned.1.call-start = ((), (), s32[]{:S(2)}) async-start(), calls=%async_computation.1 | async-start | bytes 2097152 | tf_op jit(solution)/shard_map/psum | solution.py:98
  120.1 92.1 %all-reduce.9.cloned.1.call-start = ((), (), s32[]{:S(2)}) async-start(), calls=%async_computation.2 | async-start | bytes 2097152 | tf_op jit(solution)/shard_map/psum | solution.py:96
  153.1 2.1 copy-start.14
  153.1 3.1 %copy-start.12 = (bf16[2,2048,512]{2,1,0:T(8,128)(2,1)S(1)}, bf16[2,2048,512]{2,1,0:T(8,128)(2,1)}, u32[]{:S(2)}) copy-start(bf16[2,2048,512]{2,1,0:T(8,128)(2,1)} %param.18) | copy-start | bytes 12582916
  157.1 1.7 copy-start.10
  167.0 4.2 %copy-start.7 = (f32[256,2,128]{2,1,0:T(2,128)S(1)}, f32[256,2,128]{2,1,0:T(2,128)}, u32[]{:S(2)}) copy-start(f32[256,2,128]{2,1,0:T(2,128)} %copy.59) | copy-start | bytes 786436
  177.6 3.4 %copy-start.6 = (bf16[256,256]{0,1:T(8,128)(2,1)S(1)}, bf16[256,256]{0,1:T(8,128)(2,1)}, u32[]{:S(2)}) copy-start(bf16[256,256]{0,1:T(8,128)(2,1)} %copy-done.5) | copy-start | bytes 393220
  177.6 3.6 %copy-start.2 = (bf16[256,2,64]{0,2,1:T(8,128)(2,1)S(1)}, bf16[256,2,64]{0,2,1:T(8,128)(2,1)}, u32[]{:S(2)}) copy-start(bf16[256,2,64]{0,2,1:T(8,128)(2,1)} %copy-done.1) | copy-start | bytes 196612
  177.6 3.6 %copy-start.4 = (bf16[256,2,64]{0,2,1:T(8,128)(2,1)S(1)}, bf16[256,2,64]{0,2,1:T(8,128)(2,1)}, u32[]{:S(2)}) copy-start(bf16[256,2,64]{0,2,1:T(8,128)(2,1)} %copy-done.3) | copy-start | bytes 196612
  181.0 103.1 %all-reduce.11.cloned.1.call-start = ((), (), s32[]{:S(2)}) async-start(), calls=%async_computation.3 | async-start | bytes 2097152 | tf_op jit(solution)/shard_map/psum | solution.py:98
  220.7 11.8 %copy-start.8 = (pred[256,64]{1,0:T(8,128)(4,1)S(1)}, pred[256,64]{1,0:T(8,128)(4,1)}, u32[]{:S(2)}) copy-start(pred[256,64]{1,0:T(8,128)(4,1)} %get-tuple-element.33) | copy-start | bytes 49156
Sparse Core Ops, SparseCore 0:
  67.4 33.6 all-reduce.4
  120.3 31.0 all-reduce.6
  181.1 31.0 all-reduce.8
  232.7 31.0 all-reduce.10
where the time goes:
time: 298 us; the launch traced here: 293 us
  waiting for transfers between devices  95.1 us (32%)
  matrix products  73.9 us (25%)
  other arithmetic  71.4 us (24%)
  local copies, waits for them, and re-layouts  37.6 us (13%)
  between operations  14.6 us (5%)
    psum x4, waiting for transfers between devices, local_step(): hidden = hidden + lax.psum(part_out, 'tp')  95 us
    select_n x1, other arithmetic, write_rows(): return jnp.where(at_pos, rows[:, :, None], cache)  51.5 us
    dot_general x2, matrix products, mlp_block(): jnp.dot(activated, wd_layer, preferred_element_type=jnp.float32)  23.3 us
    slice x1, local copies, waits for them, and re-layouts, local_step(): k_cache[layer]  16.5 us
    slice x1, local copies, waits for them, and re-layouts, local_step(): v_cache[layer]  16.2 us
    dot_general x2, matrix products, attend_split(): jnp.einsum('bkgd,bskd->bkgs', query, k_old, preferred_element_type=jnp.fl...  13.4 us
    dot_general x2, matrix products, mlp_block(): jnp.dot(normed, wg_layer, preferred_element_type=jnp.float32)  12.5 us
    dot_general x2, matrix products, attend_split(): jnp.einsum('bkgs,bskd->bkgd', prob_old, v_old, preferred_element_type=jnp...  9.26 us
  transfers between devices with their start and end apart: 4, of which 3 were waited for; matrix products, arithmetic and copies ran while one was open for 18% of the time, Pallas kernels for 0%

commit v1 on v0

v1 whole, which is shorter than its diff:
```python
import functools
import math

import jax
import jax.numpy as jnp
import numpy as np
from jax import lax
from jax.experimental import pallas as pl
from jax.experimental.pallas import tpu as pltpu
from jax.sharding import PartitionSpec as P

MESH = pl.DeviceIdType.MESH
BF16 = jnp.bfloat16
F32 = jnp.float32
ANY = pl.BlockSpec(memory_space=pl.ANY)
VMEM = pl.BlockSpec(memory_space=pltpu.VMEM)
SMEM = pl.BlockSpec(memory_space=pltpu.SMEM)


def rope_by_position(seq_len, head_dim):
    half = head_dim // 2
    inv_freq = np.power(np.float32(500000.0), -np.arange(half, dtype=np.float32) * np.float32(2.0 / head_dim)).astype(np.float32)
    wavelen = np.float32(2.0 * math.pi) / inv_freq
    smooth = (np.float32(8192.0) / wavelen - np.float32(1.0)) / np.float32(3.0)
    blended = (np.float32(1.0) - smooth) * inv_freq / np.float32(8.0) + smooth * inv_freq
    scaled = np.where(wavelen < 2048.0, inv_freq, np.where(wavelen > 8192.0, inv_freq / np.float32(8.0), blended)).astype(np.float32)
    angles = np.arange(seq_len, dtype=np.float32)[:, None] * scaled[None, :]
    cos = np.cos(angles.astype(np.float64)).astype(np.float32)
    sin = np.sin(angles.astype(np.float64)).astype(np.float32)
    return np.concatenate([cos, cos], axis=1), np.concatenate([-sin, sin], axis=1)


def rms(rows_f32, weight_f32):
    mean_sq = jnp.mean(rows_f32 * rows_f32, axis=-1, keepdims=True)
    return (rows_f32 * lax.rsqrt(mean_sq + 1e-5) * weight_f32).astype(BF16)


def attention_kernel(layer, first, chunk, *refs):
    refs = list(refs)
    pos_ref = refs.pop(0)
    x_ref = refs.pop(0)
    norm_ref = refs.pop(0) if first else None
    cos_tab, sin_tab, wq_hbm, wk_hbm, wv_hbm, wo_hbm, kc_hbm, vc_hbm = refs[:8]
    refs = refs[8:]
    if not first:
        refs = refs[2:]
    part_ref, ko_hbm, vo_hbm = refs[:3]
    (wq, wk, wv, wo, kbuf, vbuf, h_scr, cos_scr, sin_scr, lim_scr, q_scr, k_scr, v_scr, kb_scr, vb_scr, s_scr, p_scr, o_scr,
     w_sem, in_sem, out_sem) = refs[3:]
    batch = x_ref.shape[0]
    n_q = wq.shape[1] // 128
    n_kv = wk.shape[1] // 128
    group = n_q // n_kv
    seq = kbuf.shape[1]
    n_chunks = batch // chunk

    loads = []
    for i, (src, dst) in enumerate(((wq_hbm, wq), (wk_hbm, wk), (wv_hbm, wv))):
        loads.append(pltpu.make_async_copy(src.at[layer], dst, w_sem.at[i]))
    for c in loads:
        c.start()
    kv_loads = []
    for c in range(n_chunks):
        rows = pl.ds(c * chunk, chunk)
        a = pltpu.make_async_copy(kc_hbm.at[layer, rows], kbuf.at[rows], in_sem.at[0, c])
        b = pltpu.make_async_copy(vc_hbm.at[layer, rows], vbuf.at[rows], in_sem.at[1, c])
        a.start()
        b.start()
        kv_loads.append((a, b))
    wo_load = pltpu.make_async_copy(wo_hbm.at[layer], wo, w_sem.at[3])
    wo_load.start()

    if first:
        weight = norm_ref[layer:layer + 1, :].astype(F32)

        def norm_body(i, carry):
            rows = pl.ds(pl.multiple_of(i * 16, 16), 16)
            h_scr[rows, :] = rms(x_ref[rows, :].astype(F32), weight)
            return carry

        lax.fori_loop(0, batch // 16, norm_body, 0)
        h_src = h_scr
    else:
        h_src = x_ref

    lane_head = lax.broadcasted_iota(jnp.int32, (n_q, 128), 1) % n_kv
    row_head = lax.broadcasted_iota(jnp.int32, (n_q, 128), 0) // group
    same_head = lane_head == row_head

    def table_body(i, carry):
        for u in range(8):
            b = i * 8 + u
            pos = pos_ref[b]
            cos_scr[pl.ds(b, 1), :] = cos_tab[pl.ds(pos, 1), :]
            sin_scr[pl.ds(b, 1), :] = sin_tab[pl.ds(pos, 1), :]
            lim_scr[pl.ds(b * n_q, n_q), :] = jnp.where(same_head, pos * n_kv + n_kv - 1, -1)
        return carry

    lax.fori_loop(0, batch // 8, table_body, 0)

    def rope(v):
        v = v.astype(BF16).astype(F32)
        return v * cos_scr[...] + pltpu.roll(v, 64, 1) * sin_scr[...]

    h = h_src[...]
    loads[0].wait()
    q = jnp.dot(h, wq[...], preferred_element_type=F32)
    for j in range(n_q):
        q_scr[pl.ds(j, batch, n_q), :] = rope(q[:, j * 128:(j + 1) * 128])
    loads[1].wait()
    k = jnp.dot(h, wk[...], preferred_element_type=F32)
    for j in range(n_kv):
        k_scr[pl.ds(j, batch, n_kv), :] = rope(k[:, j * 128:(j + 1) * 128])
    loads[2].wait()
    v = jnp.dot(h, wv[...], preferred_element_type=F32)
    for j in range(n_kv):
        v_scr[pl.ds(j, batch, n_kv), :] = v[:, j * 128:(j + 1) * 128]
    kb_scr.reshape(batch * n_kv, 128)[...] = k_scr[...].astype(BF16)
    vb_scr.reshape(batch * n_kv, 128)[...] = v_scr[...].astype(BF16)

    rows_kv = seq * n_kv
    kmat = kbuf.reshape(batch * rows_kv, 128)
    vmat = vbuf.reshape(batch * rows_kv, 128)
    scale = 128 ** -0.5
    row_id = lax.broadcasted_iota(jnp.int32, (4 * n_q, 128), 0)
    first_pair = row_id < 2 * n_q
    first_in_pair = (row_id % (2 * n_q)) < n_q
    zero = jnp.zeros((4 * n_q, 128), F32)
    quads = chunk // 4
    srows = chunk * n_q

    def square(mat, base):
        top = mat[pl.ds(base, 2 * rows_kv), :]
        bottom = mat[pl.ds(base + 2 * rows_kv, 2 * rows_kv), :]
        return jnp.concatenate([top, bottom], axis=1)

    stores = []
    for c in range(n_chunks):
        rows = pl.ds(c * chunk, chunk)
        stores.append((pltpu.make_async_copy(kbuf.at[rows], ko_hbm.at[layer, rows], out_sem.at[0, c]),
                       pltpu.make_async_copy(vbuf.at[rows], vo_hbm.at[layer, rows], out_sem.at[1, c])))

    for c in range(n_chunks):
        kv_loads[c][0].wait()
        kv_loads[c][1].wait()

        def insert_body(i, carry):
            for u in range(8):
                b = c * chunk + i * 8 + u
                pos = pos_ref[b]
                kbuf[b, pos] = kb_scr[b]
                vbuf[b, pos] = vb_scr[b]
            return carry

        lax.fori_loop(0, chunk // 8, insert_body, 0)

        for t in range(quads):
            b = c * chunk + t * 4
            q4 = q_scr[pl.ds(b * n_q, 4 * n_q), :]
            wide = jnp.concatenate([jnp.where(first_pair, q4, zero), jnp.where(first_pair, zero, q4)], axis=1).astype(BF16)
            s = lax.dot_general(wide, square(kmat, b * rows_kv), (((1,), (1,)), ((), ())), preferred_element_type=F32)
            s_scr[pl.ds(t * 4 * n_q, 4 * n_q), :] = jnp.where(first_in_pair, s[:, :rows_kv], s[:, rows_kv:])
        lanes = lax.broadcasted_iota(jnp.int32, (srows, 128), 1)
        s = jnp.where(lanes <= lim_scr[pl.ds(c * srows, srows), :], s_scr[...] * scale, -jnp.inf)
        e = jnp.exp(s - jnp.max(s, axis=-1, keepdims=True))
        p_scr[...] = (e * (1.0 / jnp.sum(e, axis=-1, keepdims=True)))
        for t in range(quads):
            b = c * chunk + t * 4
            p4 = p_scr[pl.ds(t * 4 * n_q, 4 * n_q), :]
            wide = jnp.concatenate([jnp.where(first_in_pair, p4, zero), jnp.where(first_in_pair, zero, p4)], axis=1).astype(BF16)
            o = jnp.dot(wide, square(vmat, b * rows_kv), preferred_element_type=F32)
            o_scr[pl.ds(b * n_q, 4 * n_q), :] = jnp.where(first_pair, o[:, :128], o[:, 128:])
        stores[c][0].start()
        stores[c][1].start()

    att = jnp.concatenate([o_scr[pl.ds(j, batch, n_q), :].astype(BF16) for j in range(n_q)], axis=1)
    wo_load.wait()
    for n in range(wo.shape[1] // 512):
        cols = pl.ds(n * 512, 512)
        part_ref[:, cols] = jnp.dot(att, wo[:, cols], preferred_element_type=F32).astype(BF16)
    for a, b in stores:
        a.wait()
        b.wait()


def attention_call(layer, first, positions, x, norm, tables, wq, wk, wv, wo, kc, vc, k_out, v_out):
    batch, d = x.shape
    _, _, seq, n_kv, hd = kc.shape
    n_q = wq.shape[2] // hd
    chunk = 64
    n_chunks = batch // chunk
    ins = [positions, x] + ([norm] if first else []) + [tables[0], tables[1], wq, wk, wv, wo, kc, vc]
    specs = [SMEM, VMEM] + ([VMEM] if first else []) + [VMEM, VMEM] + [ANY] * 6
    aliases = {}
    if not first:
        aliases = {len(ins): 1, len(ins) + 1: 2}
        ins += [k_out, v_out]
        specs += [ANY, ANY]
    scratch = [
        pltpu.VMEM(wq.shape[1:], BF16), pltpu.VMEM(wk.shape[1:], BF16), pltpu.VMEM(wv.shape[1:], BF16), pltpu.VMEM(wo.shape[1:], BF16),
        pltpu.VMEM(kc.shape[1:], BF16), pltpu.VMEM(vc.shape[1:], BF16),
        pltpu.VMEM((batch if first else 16, d), BF16),
        pltpu.VMEM((batch, hd), F32), pltpu.VMEM((batch, hd), F32), pltpu.VMEM((batch * n_q, hd), jnp.int32),
        pltpu.VMEM((batch * n_q, hd), F32), pltpu.VMEM((batch * n_kv, hd), F32), pltpu.VMEM((batch * n_kv, hd), F32),
        pltpu.VMEM((batch, n_kv, hd), BF16), pltpu.VMEM((batch, n_kv, hd), BF16),
        pltpu.VMEM((chunk * n_q, hd), F32), pltpu.VMEM((chunk * n_q, hd), F32), pltpu.VMEM((batch * n_q, hd), F32),
        pltpu.SemaphoreType.DMA((4,)), pltpu.SemaphoreType.DMA((2, n_chunks)), pltpu.SemaphoreType.DMA((2, n_chunks)),
    ]
    return pl.pallas_call(
        functools.partial(attention_kernel, layer, first, chunk),
        out_shape=(jax.ShapeDtypeStruct((batch, d), BF16), jax.ShapeDtypeStruct(kc.shape, BF16), jax.ShapeDtypeStruct(vc.shape, BF16)),
        in_specs=specs,
        out_specs=(VMEM, ANY, ANY),
        scratch_shapes=scratch,
        input_output_aliases=aliases,
        compiler_params=pltpu.CompilerParams(vmem_limit_bytes=56 * 2**20),
        name=f"attention{layer}",
    )(*ins)


GROUPS = 2
SUB = 2
NCOL = 4


def mlp_kernel(layer, last, x_ref, part_ref, norm_ref, next_norm_ref, wg_hbm, wu_hbm, wd_hbm, *refs):
    if last:
        (xo_ref,), refs = refs[:1], refs[1:]
    else:
        (ho_ref, xo_ref), refs = refs[:2], refs[2:]
    (wg, wu, wd, d1, c1, x1, d2, c2, x2, x_own, hbuf, abuf, pbuf, obuf, w_sem, s_send, s_recv) = refs
    t = lax.axis_index("tp")
    core = lax.rem(t, 2)
    other = 1 - core
    partner = t + other - core
    across = lax.rem(t + 2, 4)
    d = x_ref.shape[1]
    half = d1.shape[0]
    rows_g = half // GROUPS
    rows_s = rows_g // SUB
    cols_n = d // NCOL

    barrier = pltpu.get_barrier_semaphore()
    for dev in (partner, across):
        pl.semaphore_signal(barrier, inc=1, device_id={"tp": dev}, device_id_type=MESH)
    w_loads = []
    for i, (src, dst) in enumerate(((wg_hbm, wg), (wu_hbm, wu), (wd_hbm, wd))):
        n = dst.shape[0] // 4
        for j in range(4):
            cp = pltpu.make_async_copy(src.at[layer, pl.ds(j * n, n)], dst.at[pl.ds(j * n, n)], w_sem.at[i, j])
            cp.start()
            w_loads.append(cp)
    pl.semaphore_wait(barrier, 2)

    def send(stage, idx, src, dst, dev):
        cp = pltpu.make_async_remote_copy(src_ref=src, dst_ref=dst, send_sem=s_send.at[stage, idx], recv_sem=s_recv.at[stage, idx],
                                          device_id={"tp": dev}, device_id_type=MESH)
        cp.start()
        return cp

    started = []

    subs = [(g, s, g * rows_g + s * rows_s) for g in range(GROUPS) for s in range(SUB)]
    near = []
    for i, (g, s, r0) in enumerate(subs):
        near.append(send(0, i, part_ref.at[pl.ds(other * half + r0, rows_s)], d1.at[pl.ds(r0, rows_s)], partner))
    far = []
    for i, (g, s, r0) in enumerate(subs):
        near[i].wait_recv()
        rows = pl.ds(r0, rows_s)
        c1[rows, :] = (part_ref[pl.ds(core * half + r0, rows_s), :].astype(F32) + d1[rows, :].astype(F32)).astype(BF16)
        far.append(send(1, i, c1.at[rows], x1.at[rows], across))
    started += near + far

    weight = norm_ref[layer:layer + 1, :].astype(F32)
    gathers1 = {}

    def finish1(g):
        for s in range(SUB):
            i = g * SUB + s
            far[i].wait_recv()
            for r in range(rows_s // 16):
                r0 = g * rows_g + s * rows_s + r * 16
                rows = pl.ds(r0, 16)
                total = (c1[rows, :].astype(F32) + x1[rows, :].astype(F32)).astype(BF16)
                res = x_ref[pl.ds(r0, 16), :] if last else x_ref[pl.ds(core * half + r0, 16), :]
                xn = (res.astype(F32) + total.astype(F32)).astype(BF16)
                x_own[rows, :] = xn
                hbuf[g, core, pl.ds(s * rows_s + r * 16, 16), :] = rms(xn.astype(F32), weight)
            part = hbuf.at[g, core, pl.ds(s * rows_s, rows_s)]
            cp = send(2, i, part, part, partner)
            gathers1[i] = cp
            started.append(cp)

    def wait1(g):
        for s in range(SUB):
            gathers1[g * SUB + s].wait_recv()

    def gate_up(g):
        hid = hbuf.at[g].reshape(2 * rows_g, d)

        def body(n, carry):
            cols = pl.ds(pl.multiple_of(n * 512, 512), 512)
            gate = jnp.dot(hid[...], wg[:, cols], preferred_element_type=F32).astype(BF16).astype(F32)
            up = jnp.dot(hid[...], wu[:, cols], preferred_element_type=F32).astype(BF16).astype(F32)
            abuf[:, cols] = (gate * (1.0 / (1.0 + jnp.exp(-gate))) * up).astype(BF16)
            return carry

        lax.fori_loop(0, wg.shape[1] // 512, body, 0)

    near2, far2 = {}, {}

    def relay2(g, n):
        i = g * NCOL + n
        near2[i].wait_recv()
        cols = pl.ds(n * cols_n, cols_n)
        rows = pl.ds(g * rows_g, rows_g)
        c2[rows, cols] = (pbuf[g, core, :, cols].astype(F32) + d2[rows, cols].astype(F32)).astype(BF16)
        far2[i] = send(4, i, c2.at[rows, cols], x2.at[rows, cols], across)
        started.append(far2[i])

    def down(g):
        for n in range(NCOL):
            cols = pl.ds(n * cols_n, cols_n)
            y = jnp.dot(abuf[...], wd[:, cols], preferred_element_type=F32).astype(BF16)
            pbuf[g, :, :, cols] = y.reshape(2, rows_g, cols_n)
            i = g * NCOL + n
            near2[i] = send(3, i, pbuf.at[g, other, :, cols], d2.at[pl.ds(g * rows_g, rows_g), cols], partner)
            started.append(near2[i])
            if n > 0:
                relay2(g, n - 1)
        relay2(g, NCOL - 1)

    gathers2 = {}

    def finish2(g):
        for n in range(NCOL):
            far2[g * NCOL + n].wait_recv()
        if not last:
            nweight = next_norm_ref[layer + 1:layer + 2, :].astype(F32)
        for s in range(SUB):
            for r in range(rows_s // 16):
                r0 = g * rows_g + s * rows_s + r * 16
                rows = pl.ds(r0, 16)
                total = (c2[rows, :].astype(F32) + x2[rows, :].astype(F32)).astype(BF16)
                xn = (x_own[rows, :].astype(F32) + total.astype(F32)).astype(BF16)
                if last:
                    obuf[g, core, pl.ds(s * rows_s + r * 16, 16), :] = xn
                else:
                    xo_ref[rows, :] = xn
                    obuf[g, core, pl.ds(s * rows_s + r * 16, 16), :] = rms(xn.astype(F32), nweight)
            part = obuf.at[g, core, pl.ds(s * rows_s, rows_s)]
            cp = send(5, g * SUB + s, part, part, partner)
            gathers2[g * SUB + s] = cp
            started.append(cp)

    def wait2(g):
        out = xo_ref if last else ho_ref
        for s in range(SUB):
            gathers2[g * SUB + s].wait_recv()
        for c in range(2):
            out[c * half + g * rows_g:c * half + (g + 1) * rows_g, :] = obuf[g, c]

    finish1(0)
    wait1(0)
    for cp in w_loads:
        cp.wait()
    gate_up(0)
    down(0)
    finish1(1)
    wait1(1)
    gate_up(1)
    down(1)
    finish2(0)
    wait2(0)
    finish2(1)
    wait2(1)
    for cp in started:
        cp.wait_send()


def mlp_call(layer, last, x, part, norm, next_norm, wg, wu, wd):
    batch, d = part.shape
    half = batch // 2
    rows_g = half // GROUPS
    ff = wg.shape[2]
    n_sem = max(GROUPS * NCOL, GROUPS * SUB)
    own = lambda: pltpu.VMEM((half, d), BF16)
    scratch = [
        pltpu.VMEM(wg.shape[1:], BF16), pltpu.VMEM(wu.shape[1:], BF16), pltpu.VMEM(wd.shape[1:], BF16),
        own(), own(), own(), own(), own(), own(), own(),
        pltpu.VMEM((GROUPS, 2, rows_g, d), BF16), pltpu.VMEM((2 * rows_g, ff), BF16),
        pltpu.VMEM((GROUPS, 2, rows_g, d), BF16), pltpu.VMEM((GROUPS, 2, rows_g, d), BF16),
        pltpu.SemaphoreType.DMA((3, 4)), pltpu.SemaphoreType.DMA((6, n_sem)), pltpu.SemaphoreType.DMA((6, n_sem)),
    ]
    full = jax.ShapeDtypeStruct((batch, d), BF16)
    mine = jax.ShapeDtypeStruct((half, d), BF16)
    return pl.pallas_call(
        functools.partial(mlp_kernel, layer, last),
        out_shape=full if last else (full, mine),
        in_specs=[VMEM] * 4 + [ANY] * 3,
        out_specs=VMEM if last else (VMEM, VMEM),
        scratch_shapes=scratch,
        compiler_params=pltpu.CompilerParams(collective_id=layer, has_side_effects=True, vmem_limit_bytes=48 * 2**20),
        name=f"mlp{layer}",
    )(x, part, norm, next_norm, wg, wu, wd)


def solution(mesh):
    row_spec = P('dp', None)
    pos_spec = P('dp')
    cache_spec = P(None, 'dp', None, 'tp', None)
    norm_spec = P(None, None)
    col_spec = P(None, None, 'tp')
    split_rows = P(None, 'tp', None)

    def local_step(hidden, positions, k_cache, v_cache, attn_norm, w_query, w_key, w_value, w_out, mlp_norm, w_gate, w_up, w_down):
        tables = [jnp.asarray(t) for t in rope_by_position(k_cache.shape[2], k_cache.shape[4])]
        part, k_out, v_out = attention_call(0, True, positions, hidden, attn_norm, tables, w_query, w_key, w_value, w_out, k_cache, v_cache, None, None)
        h, x_own = mlp_call(0, False, hidden, part, mlp_norm, attn_norm, w_gate, w_up, w_down)
        part, k_out, v_out = attention_call(1, False, positions, h, None, tables, w_query, w_key, w_value, w_out, k_cache, v_cache, k_out, v_out)
        hidden = mlp_call(1, True, x_own, part, mlp_norm, attn_norm, w_gate, w_up, w_down)
        return hidden, k_out, v_out

    return jax.shard_map(local_step, mesh=mesh, in_specs=(row_spec, pos_spec, cache_spec, cache_spec, norm_spec, col_spec, col_spec, col_spec, split_rows, norm_spec, col_spec, col_spec, split_rows), out_specs=(row_spec, cache_spec, cache_spec), check_vma=False)
```

time: 298 us -> 111 us (0.37); the launches traced: 293 us -> 110 us
  Pallas kernels: 0 us -> 105 us
  waiting for transfers between devices: 95.1 us -> 0 us
  matrix products: 73.9 us -> 0 us
  other arithmetic: 71.4 us -> 0 us
  local copies, waits for them, and re-layouts: 37.6 us -> 4.39 us
  between operations: 14.6 us -> 0.74 us
    pallas_call x0 -> x4, Pallas kernels: none -> 105 us  [the longest x2 69.2 us: mlp_call(): pl.pallas_call(functools.partial(mlp_kernel, layer, last), out_shape=full...]
    psum x4 -> x0, waiting for transfers between devices: 95 us -> none  [local_step(): hidden = hidden + lax.psum(part_out, 'tp')]
    dot_general x16 -> x0, matrix products: 73.9 us -> none  [the longest x2 23.3 us: mlp_block(): jnp.dot(activated, wd_layer, preferred_element_type=jnp.float32)]
    select_n x2 -> x0, other arithmetic: 51.5 us -> none  [the longest x1 51.5 us: write_rows(): return jnp.where(at_pos, rows[:, :, None], cache)]
    slice x2 -> x0, local copies, waits for them, and re-layouts: 32.7 us -> none  [the longest x1 16.5 us: local_step(): k_cache[layer]]
    reduce_sum x6 -> x0, other arithmetic: 9.79 us -> none  [the longest x4 6.7 us: rms_norm(): mean_sq = jnp.mean(hidden_f32 * hidden_f32, axis=-1, keepdims=True)]
    unnamed x32 -> x13, local copies, waits for them, and re-layouts: 1.02 us -> 4.39 us
    unnamed x4 -> x0, other arithmetic: 3.08 us -> none
  transfers between devices with their start and end apart: 4 -> 0, of which waited for: 3 -> 0; matrix products, arithmetic and copies ran while one was open for 18% -> 0% of each run, Pallas kernels for 0% -> 0%
where the time goes in v1:
time: 111 us; the launch traced here: 110 us
  Pallas kernels  105 us (95%)
  local copies, waits for them, and re-layouts  4.39 us (4%)
    pallas_call x2, Pallas kernels, mlp_call(): pl.pallas_call(functools.partial(mlp_kernel, layer, last), out_shape=full...  69.2 us
    pallas_call x2, Pallas kernels, attention_call(): pl.pallas_call(functools.partial(attention_kernel, layer, first, chunk),...  36 us
    unnamed x13, local copies, waits for them, and re-layouts  4.39 us

profile of v1, /device:TPU:0, one launch (start us, length us, event | category | flops | bytes accessed | tf_op | source)
XLA Modules:
  0.0 110.3 jit_solution(12066011516627734763)
XLA Ops:
  0.6 0.0 copy-start.4
  0.6 0.0 copy-start.5
  0.7 0.0 copy-start
  0.7 17.9 %attention0.1 = (bf16[256,2048]{1,0:T(8,128)(2,1)}, bf16[2,256,64,2,128]{4,3,2,1,0:T(2,128)(2,1)}, bf16[2,256,64,2,128]{4,3,2,1,0:T(2,128)(2,1)}) custom-call(s32[256]{0:T(256)} %refs_0_.3, bf16[256,2048]{1,0:T(8,128)(2,1)} %x_ref.1, bf16[2,2048]{1,0:T(2,128)(2,1)} %next_norm_ref.3, f32[64,128]{1,0:T(8,128)} %constant.4.clone.refs_3_.refs_2_, ...), custom_call_target="tpu_custom_call" | custom-call | tf_op jit(solution)/shard_map/attention0/pallas_call | solution.py:209
  18.6 0.0 copy-done.4
  18.6 0.0 copy-done.5
  18.6 0.0 copy-done
  18.6 0.0 copy-start.3
  18.7 1.2 %copy-done.3 = bf16[256,2048]{1,0:T(8,128)(2,1)S(1)} copy-done((bf16[256,2048]{1,0:T(8,128)(2,1)S(1)}, bf16[256,2048]{1,0:T(8,128)(2,1)}, u32[]{:S(2)}) %copy-start.3) | copy-done | bytes 1048600
  19.9 35.5 %mlp0.1 = (bf16[256,2048]{1,0:T(8,128)(2,1)S(1)}, bf16[128,2048]{1,0:T(8,128)(2,1)S(1)}) custom-call(bf16[256,2048]{1,0:T(8,128)(2,1)S(1)} %copy-done, bf16[256,2048]{1,0:T(8,128)(2,1)S(1)} %copy-done.3, bf16[2,2048]{1,0:T(2,128)(2,1)S(1)} %copy-done.5, bf16[2,2048]{1,0:T(2,128)(2,1)S(1)} %copy-done.4, bf16[2,2048,2048]{2,1,0:T(8,128)(2,1)} %wg_hbm.3, ...), custom_call_target="tpu_custom_call" | custom-call | tf_op jit(solution)/shard_map/mlp0/pallas_call | solution.py:398
  55.4 0.0 copy-start.1
  55.4 1.0 copy-done.1
  56.4 18.1 %attention1.1 = (bf16[256,2048]{1,0:T(8,128)(2,1)}, bf16[2,256,64,2,128]{4,3,2,1,0:T(2,128)(2,1)}, bf16[2,256,64,2,128]{4,3,2,1,0:T(2,128)(2,1)}) custom-call(s32[256]{0:T(256)} %refs_0_.3, bf16[256,2048]{1,0:T(8,128)(2,1)} %copy-done.1, f32[64,128]{1,0:T(8,128)} %constant.4.clone.refs_3_.refs_2_, ...), custom_call_target="tpu_custom_call", output_to_operand_aliasing={{1}: (10, {}), {2}: (11, {})} | custom-call | tf_op jit(solution)/shard_map/attention1/pallas_call | solution.py:209
  74.5 0.0 copy-start.2
  74.5 1.2 %copy-done.2 = bf16[256,2048]{1,0:T(8,128)(2,1)S(1)} copy-done((bf16[256,2048]{1,0:T(8,128)(2,1)S(1)}, bf16[256,2048]{1,0:T(8,128)(2,1)}, u32[]{:S(2)}) %copy-start.2) | copy-done | bytes 1048600
  75.7 33.6 %mlp1.1 = bf16[256,2048]{1,0:T(8,128)(2,1)S(1)} custom-call(bf16[128,2048]{1,0:T(8,128)(2,1)S(1)} %get-tuple-element.12.x_ref, bf16[256,2048]{1,0:T(8,128)(2,1)S(1)} %copy-done.2, bf16[2,2048]{1,0:T(2,128)(2,1)S(1)} %copy-done.5, bf16[2,2048]{1,0:T(2,128)(2,1)S(1)} %copy-done.4, bf16[2,2048,2048]{2,1,0:T(8,128)(2,1)} %wg_hbm.3, ...), custom_call_target="tpu_custom_call" | custom-call | tf_op jit(solution)/shard_map/mlp1/pallas_call | solution.py:398
  109.3 1.0 copy.23
Async XLA Ops:
  0.6 18.0 %copy-start.4 = (bf16[2,2048]{1,0:T(2,128)(2,1)S(1)}, bf16[2,2048]{1,0:T(2,128)(2,1)}, u32[]{:S(2)}) copy-start(bf16[2,2048]{1,0:T(2,128)(2,1)} %next_norm_ref.3) | copy-start | bytes 24580
  0.6 18.0 %copy-start.5 = (bf16[2,2048]{1,0:T(2,128)(2,1)S(1)}, bf16[2,2048]{1,0:T(2,128)(2,1)}, u32[]{:S(2)}) copy-start(bf16[2,2048]{1,0:T(2,128)(2,1)} %norm_ref.3) | copy-start | bytes 24580
  0.7 18.0 %copy-start = (bf16[256,2048]{1,0:T(8,128)(2,1)S(1)}, bf16[256,2048]{1,0:T(8,128)(2,1)}, u32[]{:S(2)}) copy-start(bf16[256,2048]{1,0:T(8,128)(2,1)} %x_ref.1) | copy-start | bytes 3145732
  18.6 1.2 %copy-start.3 = (bf16[256,2048]{1,0:T(8,128)(2,1)S(1)}, bf16[256,2048]{1,0:T(8,128)(2,1)}, u32[]{:S(2)}) copy-start(bf16[256,2048]{1,0:T(8,128)(2,1)} %get-tuple-element.11.part_ref) | copy-start | bytes 3145732
  55.4 1.0 copy-start.1
  74.5 1.2 %copy-start.2 = (bf16[256,2048]{1,0:T(8,128)(2,1)S(1)}, bf16[256,2048]{1,0:T(8,128)(2,1)}, u32[]{:S(2)}) copy-start(bf16[256,2048]{1,0:T(8,128)(2,1)} %get-tuple-element.16.part_ref) | copy-start | bytes 3145732

commit v2 on v1

--- a/solution.py
+++ b/solution.py
@@ -13,6 +13,7 @@
 BF16 = jnp.bfloat16
 F32 = jnp.float32
 ANY = pl.BlockSpec(memory_space=pl.ANY)
+HBM = pl.BlockSpec(memory_space=pltpu.HBM)
 VMEM = pl.BlockSpec(memory_space=pltpu.VMEM)
 SMEM = pl.BlockSpec(memory_space=pltpu.SMEM)
 
@@ -35,18 +36,26 @@
     return (rows_f32 * lax.rsqrt(mean_sq + 1e-5) * weight_f32).astype(BF16)
 
 
+def in_hbm(arrays):
+    return [pltpu.with_memory_space_constraint(a, pltpu.HBM) for a in arrays]
+
+
 def attention_kernel(layer, first, chunk, *refs):
     refs = list(refs)
     pos_ref = refs.pop(0)
-    x_ref = refs.pop(0)
+    x_in = refs.pop(0)
     norm_ref = refs.pop(0) if first else None
     cos_tab, sin_tab, wq_hbm, wk_hbm, wv_hbm, wo_hbm, kc_hbm, vc_hbm = refs[:8]
     refs = refs[8:]
-    if not first:
-        refs = refs[2:]
-    part_ref, ko_hbm, vo_hbm = refs[:3]
-    (wq, wk, wv, wo, kbuf, vbuf, h_scr, cos_scr, sin_scr, lim_scr, q_scr, k_scr, v_scr, kb_scr, vb_scr, s_scr, p_scr, o_scr,
-     w_sem, in_sem, out_sem) = refs[3:]
+    if first:
+        part_ref, ko_hbm, vo_hbm = refs[:3]
+        x_ref, wq, wk, wv, wo, kbuf, vbuf, h_scr = refs[3:11]
+        refs = refs[11:]
+    else:
+        x_ref, wq, wk, wv, wo = x_in, wq_hbm, wk_hbm, wv_hbm, wo_hbm
+        part_ref, ko_hbm, vo_hbm, kbuf, vbuf = refs[2:7]
+        refs = refs[7:]
+    (cos_scr, sin_scr, lim_scr, q_scr, k_scr, v_scr, kb_scr, vb_scr, p_scr, o_scr, w_sem, in_sem, out_sem) = refs
     batch = x_ref.shape[0]
     n_q = wq.shape[1] // 128
     n_kv = wk.shape[1] // 128
@@ -54,23 +63,43 @@
     seq = kbuf.shape[1]
     n_chunks = batch // chunk
 
-    loads = []
-    for i, (src, dst) in enumerate(((wq_hbm, wq), (wk_hbm, wk), (wv_hbm, wv))):
-        loads.append(pltpu.make_async_copy(src.at[layer], dst, w_sem.at[i]))
-    for c in loads:
-        c.start()
-    kv_loads = []
-    for c in range(n_chunks):
-        rows = pl.ds(c * chunk, chunk)
-        a = pltpu.make_async_copy(kc_hbm.at[layer, rows], kbuf.at[rows], in_sem.at[0, c])
-        b = pltpu.make_async_copy(vc_hbm.at[layer, rows], vbuf.at[rows], in_sem.at[1, c])
-        a.start()
-        b.start()
-        kv_loads.append((a, b))
-    wo_load = pltpu.make_async_copy(wo_hbm.at[layer], wo, w_sem.at[3])
-    wo_load.start()
-
-    if first:
+    if first:
+        x_load = pltpu.make_async_copy(x_in, x_ref, w_sem.at[4])
+        x_load.start()
+        loads = []
+        for i, (src, dst) in enumerate(((wq_hbm, wq), (wk_hbm, wk), (wv_hbm, wv))):
+            loads.append(pltpu.make_async_copy(src.at[layer], dst, w_sem.at[i]))
+        for c in loads:
+            c.start()
+        kv_loads = []
+        for c in range(n_chunks):
+            rows = pl.ds(c * chunk, chunk)
+            a = pltpu.make_async_copy(kc_hbm.at[layer, rows], kbuf.at[rows], in_sem.at[0, c])
+            b = pltpu.make_async_copy(vc_hbm.at[layer, rows], vbuf.at[rows], in_sem.at[1, c])
+            a.start()
+            b.start()
+            kv_loads.append((a, b))
+        wo_load = pltpu.make_async_copy(wo_hbm.at[layer], wo, w_sem.at[3])
+        wo_load.start()
+
+    per_row = 128 // n_q
+    lane_request = lax.broadcasted_iota(jnp.int32, (1, 128), 1) // n_q
+
+    def table_body(i, carry):
+        limit = jnp.zeros((1, 128), jnp.int32)
+        for u in range(per_row):
+            b = i * per_row + u
+            pos = pos_ref[b]
+            cos_scr[pl.ds(b, 1), :] = cos_tab[pl.ds(pos, 1), :]
+            sin_scr[pl.ds(b, 1), :] = sin_tab[pl.ds(pos, 1), :]
+            limit = jnp.where(lane_request == u, pos * n_kv + n_kv - 1, limit)
+        lim_scr[pl.ds(i, 1), :] = limit
+        return carry
+
+    lax.fori_loop(0, batch // per_row, table_body, 0)
+
+    if first:
+        x_load.wait()
         weight = norm_ref[layer:layer + 1, :].astype(F32)
 
         def norm_body(i, carry):
@@ -83,35 +112,23 @@
     else:
         h_src = x_ref
 
-    lane_head = lax.broadcasted_iota(jnp.int32, (n_q, 128), 1) % n_kv
-    row_head = lax.broadcasted_iota(jnp.int32, (n_q, 128), 0) // group
-    same_head = lane_head == row_head
-
-    def table_body(i, carry):
-        for u in range(8):
-            b = i * 8 + u
-            pos = pos_ref[b]
-            cos_scr[pl.ds(b, 1), :] = cos_tab[pl.ds(pos, 1), :]
-            sin_scr[pl.ds(b, 1), :] = sin_tab[pl.ds(pos, 1), :]
-            lim_scr[pl.ds(b * n_q, n_q), :] = jnp.where(same_head, pos * n_kv + n_kv - 1, -1)
-        return carry
-
-    lax.fori_loop(0, batch // 8, table_body, 0)
-
     def rope(v):
         v = v.astype(BF16).astype(F32)
         return v * cos_scr[...] + pltpu.roll(v, 64, 1) * sin_scr[...]
 
     h = h_src[...]
-    loads[0].wait()
+    if first:
+        loads[0].wait()
     q = jnp.dot(h, wq[...], preferred_element_type=F32)
     for j in range(n_q):
         q_scr[pl.ds(j, batch, n_q), :] = rope(q[:, j * 128:(j + 1) * 128])
-    loads[1].wait()
+    if first:
+        loads[1].wait()
     k = jnp.dot(h, wk[...], preferred_element_type=F32)
     for j in range(n_kv):
         k_scr[pl.ds(j, batch, n_kv), :] = rope(k[:, j * 128:(j + 1) * 128])
-    loads[2].wait()
+    if first:
+        loads[2].wait()
     v = jnp.dot(h, wv[...], preferred_element_type=F32)
     for j in range(n_kv):
         v_scr[pl.ds(j, batch, n_kv), :] = v[:, j * 128:(j + 1) * 128]
@@ -122,12 +139,20 @@
     kmat = kbuf.reshape(batch * rows_kv, 128)
     vmat = vbuf.reshape(batch * rows_kv, 128)
     scale = 128 ** -0.5
-    row_id = lax.broadcasted_iota(jnp.int32, (4 * n_q, 128), 0)
-    first_pair = row_id < 2 * n_q
-    first_in_pair = (row_id % (2 * n_q)) < n_q
-    zero = jnp.zeros((4 * n_q, 128), F32)
+    pair = 2 * n_q
+    row_id = lax.broadcasted_iota(jnp.int32, (2 * pair, 128), 0)
+    first_pair = row_id < pair
+    first_in_pair = (row_id % pair) < n_q
+    zero = jnp.zeros((2 * pair, 128), F32)
     quads = chunk // 4
-    srows = chunk * n_q
+    cols = chunk * n_q
+    lane = lax.broadcasted_iota(jnp.int32, (rows_kv, cols), 1)
+    row = lax.broadcasted_iota(jnp.int32, (rows_kv, cols), 0)
+    same_head = (row % n_kv) == (lane % n_q) // group
+    first_of_two = (lane // n_q) % 2 == 0
+    lane_pair = lax.broadcasted_iota(jnp.int32, (128, 128), 1) // pair
+    no_tile = jnp.zeros((128, 128), BF16)
+    pairs_per_tile = 128 // pair
 
     def square(mat, base):
         top = mat[pl.ds(base, 2 * rows_kv), :]
@@ -141,8 +166,9 @@
                        pltpu.make_async_copy(vbuf.at[rows], vo_hbm.at[layer, rows], out_sem.at[1, c])))
 
     for c in range(n_chunks):
-        kv_loads[c][0].wait()
-        kv_loads[c][1].wait()
+        if first:
+            kv_loads[c][0].wait()
+            kv_loads[c][1].wait()
 
         def insert_body(i, carry):
             for u in range(8):
@@ -154,30 +180,38 @@
 
         lax.fori_loop(0, chunk // 8, insert_body, 0)
 
+        q_t = q_scr[pl.ds(c * cols, cols), :].T
+        acc = None
+        for t in range(quads):
+            halves = []
+            for i in range(2):
+                p = 2 * t + i
+                tile = p // pairs_per_tile
+                tiles = [no_tile] * (cols // 128)
+                tiles[tile] = jnp.where(lane_pair == p % pairs_per_tile, q_t[:, tile * 128:(tile + 1) * 128], 0.0).astype(BF16)
+                halves.append(jnp.concatenate(tiles, axis=1))
+            d = jnp.dot(square(kmat, (c * chunk + t * 4) * rows_kv), jnp.concatenate(halves, axis=0), preferred_element_type=F32)
+            acc = d if acc is None else acc + d
+        stores[c][0].start()
+        stores[c][1].start()
+        s = jnp.where(first_of_two, acc[:rows_kv], acc[rows_kv:])
+        limit = jnp.concatenate([lim_scr[pl.ds(c * (cols // 128) + j, 1), :] for j in range(cols // 128)], axis=1)
+        s = jnp.where(same_head & (row <= limit), s * scale, -jnp.inf)
+        e = jnp.exp(s - jnp.max(s, axis=0, keepdims=True))
+        p_scr[...] = (e * (1.0 / jnp.sum(e, axis=0, keepdims=True))).T
         for t in range(quads):
             b = c * chunk + t * 4
-            q4 = q_scr[pl.ds(b * n_q, 4 * n_q), :]
-            wide = jnp.concatenate([jnp.where(first_pair, q4, zero), jnp.where(first_pair, zero, q4)], axis=1).astype(BF16)
-            s = lax.dot_general(wide, square(kmat, b * rows_kv), (((1,), (1,)), ((), ())), preferred_element_type=F32)
-            s_scr[pl.ds(t * 4 * n_q, 4 * n_q), :] = jnp.where(first_in_pair, s[:, :rows_kv], s[:, rows_kv:])
-        lanes = lax.broadcasted_iota(jnp.int32, (srows, 128), 1)
-        s = jnp.where(lanes <= lim_scr[pl.ds(c * srows, srows), :], s_scr[...] * scale, -jnp.inf)
-        e = jnp.exp(s - jnp.max(s, axis=-1, keepdims=True))
-        p_scr[...] = (e * (1.0 / jnp.sum(e, axis=-1, keepdims=True)))
-        for t in range(quads):
-            b = c * chunk + t * 4
-            p4 = p_scr[pl.ds(t * 4 * n_q, 4 * n_q), :]
+            p4 = p_scr[pl.ds(t * 2 * pair, 2 * pair), :]
             wide = jnp.concatenate([jnp.where(first_in_pair, p4, zero), jnp.where(first_in_pair, zero, p4)], axis=1).astype(BF16)
             o = jnp.dot(wide, square(vmat, b * rows_kv), preferred_element_type=F32)
-            o_scr[pl.ds(b * n_q, 4 * n_q), :] = jnp.where(first_pair, o[:, :128], o[:, 128:])
-        stores[c][0].start()
-        stores[c][1].start()
+            o_scr[pl.ds(b * n_q, 2 * pair), :] = jnp.where(first_pair, o[:, :128], o[:, 128:])
 
     att = jnp.concatenate([o_scr[pl.ds(j, batch, n_q), :].astype(BF16) for j in range(n_q)], axis=1)
-    wo_load.wait()
+    if first:
+        wo_load.wait()
     for n in range(wo.shape[1] // 512):
-        cols = pl.ds(n * 512, 512)
-        part_ref[:, cols] = jnp.dot(att, wo[:, cols], preferred_element_type=F32).astype(BF16)
+        cols_n = pl.ds(n * 512, 512)
+        part_ref[:, cols_n] = jnp.dot(att, wo[:, cols_n], preferred_element_type=F32).astype(BF16)
     for a, b in stores:
         a.wait()
         b.wait()
@@ -185,35 +219,43 @@
 
 def attention_call(layer, first, positions, x, norm, tables, wq, wk, wv, wo, kc, vc, k_out, v_out):
     batch, d = x.shape
-    _, _, seq, n_kv, hd = kc.shape
-    n_q = wq.shape[2] // hd
+    seq, n_kv, hd = kc.shape[-3:]
+    n_q = wq.shape[-1] // hd
     chunk = 64
     n_chunks = batch // chunk
-    ins = [positions, x] + ([norm] if first else []) + [tables[0], tables[1], wq, wk, wv, wo, kc, vc]
-    specs = [SMEM, VMEM] + ([VMEM] if first else []) + [VMEM, VMEM] + [ANY] * 6
-    aliases = {}
-    if not first:
-        aliases = {len(ins): 1, len(ins) + 1: 2}
-        ins += [k_out, v_out]
-        specs += [ANY, ANY]
-    scratch = [
-        pltpu.VMEM(wq.shape[1:], BF16), pltpu.VMEM(wk.shape[1:], BF16), pltpu.VMEM(wv.shape[1:], BF16), pltpu.VMEM(wo.shape[1:], BF16),
-        pltpu.VMEM(kc.shape[1:], BF16), pltpu.VMEM(vc.shape[1:], BF16),
-        pltpu.VMEM((batch if first else 16, d), BF16),
-        pltpu.VMEM((batch, hd), F32), pltpu.VMEM((batch, hd), F32), pltpu.VMEM((batch * n_q, hd), jnp.int32),
+    if first:
+        ins = [positions] + in_hbm([x]) + [norm, tables[0], tables[1]] + in_hbm([wq, wk, wv, wo, kc, vc])
+    else:
+        ins = [positions, x, tables[0], tables[1], wq, wk, wv, wo, kc, vc]
+    part = pltpu.VMEM((batch, d), BF16)
+    if first:
+        specs = [SMEM, HBM, VMEM, VMEM, VMEM] + [HBM] * 6
+        outs = (part, pltpu.HBM(kc.shape, BF16), pltpu.HBM(vc.shape, BF16))
+        out_specs = (VMEM, HBM, HBM)
+        aliases = {}
+        big = [(batch, d), wq.shape[1:], wk.shape[1:], wv.shape[1:], wo.shape[1:], kc.shape[1:], vc.shape[1:], (batch, d)]
+    else:
+        specs = [SMEM, VMEM, VMEM, VMEM] + [VMEM] * 6 + [HBM] * 2
+        aliases = {len(ins): 1, len(ins) + 1: 2, len(ins) - 2: 3, len(ins) - 1: 4}
+        outs = (part, pltpu.HBM(k_out.shape, BF16), pltpu.HBM(v_out.shape, BF16), pltpu.VMEM(kc.shape, BF16), pltpu.VMEM(vc.shape, BF16))
+        ins += in_hbm([k_out, v_out])
+        out_specs = (VMEM, HBM, HBM, VMEM, VMEM)
+        big = []
+    scratch = [pltpu.VMEM(shape, BF16) for shape in big] + [
+        pltpu.VMEM((batch, hd), F32), pltpu.VMEM((batch, hd), F32), pltpu.VMEM((batch * n_q // hd, hd), jnp.int32),
         pltpu.VMEM((batch * n_q, hd), F32), pltpu.VMEM((batch * n_kv, hd), F32), pltpu.VMEM((batch * n_kv, hd), F32),
         pltpu.VMEM((batch, n_kv, hd), BF16), pltpu.VMEM((batch, n_kv, hd), BF16),
-        pltpu.VMEM((chunk * n_q, hd), F32), pltpu.VMEM((chunk * n_q, hd), F32), pltpu.VMEM((batch * n_q, hd), F32),
-        pltpu.SemaphoreType.DMA((4,)), pltpu.SemaphoreType.DMA((2, n_chunks)), pltpu.SemaphoreType.DMA((2, n_chunks)),
+        pltpu.VMEM((chunk * n_q, hd), F32), pltpu.VMEM((batch * n_q, hd), F32),
+        pltpu.SemaphoreType.DMA((5,)), pltpu.SemaphoreType.DMA((2, n_chunks)), pltpu.SemaphoreType.DMA((2, n_chunks)),
     ]
     return pl.pallas_call(
         functools.partial(attention_kernel, layer, first, chunk),
-        out_shape=(jax.ShapeDtypeStruct((batch, d), BF16), jax.ShapeDtypeStruct(kc.shape, BF16), jax.ShapeDtypeStruct(vc.shape, BF16)),
+        out_shape=outs,
         in_specs=specs,
-        out_specs=(VMEM, ANY, ANY),
+        out_specs=out_specs,
         scratch_shapes=scratch,
         input_output_aliases=aliases,
-        compiler_params=pltpu.CompilerParams(vmem_limit_bytes=56 * 2**20),
+        compiler_params=pltpu.CompilerParams(vmem_limit_bytes=(62 if first else 8) * 2**20),
         name=f"attention{layer}",
     )(*ins)
 
@@ -225,10 +267,11 @@
 
 def mlp_kernel(layer, last, x_ref, part_ref, norm_ref, next_norm_ref, wg_hbm, wu_hbm, wd_hbm, *refs):
     if last:
+        carry_in, carry_out = (), ()
         (xo_ref,), refs = refs[:1], refs[1:]
     else:
-        (ho_ref, xo_ref), refs = refs[:2], refs[2:]
-    (wg, wu, wd, d1, c1, x1, d2, c2, x2, x_own, hbuf, abuf, pbuf, obuf, w_sem, s_send, s_recv) = refs
+        carry_in, (ho_ref, xo_ref), carry_out, refs = refs[:6], refs[6:8], refs[8:14], refs[14:]
+    (wg, wu, wd, d1, c1, x1, d2, c2, x2, x_own, hbuf, abuf, pbuf, obuf, w_sem, c_sem, s_send, s_recv) = refs
     t = lax.axis_index("tp")
     core = lax.rem(t, 2)
     other = 1 - core
@@ -250,6 +293,13 @@
             cp = pltpu.make_async_copy(src.at[layer, pl.ds(j * n, n)], dst.at[pl.ds(j * n, n)], w_sem.at[i, j])
             cp.start()
             w_loads.append(cp)
+    c_loads = []
+    for i, (src, dst) in enumerate(zip(carry_in, carry_out)):
+        n = dst.shape[0] // 4
+        for j in range(4):
+            cp = pltpu.make_async_copy(src.at[layer + 1, pl.ds(j * n, n)], dst.at[pl.ds(j * n, n)], c_sem.at[i, j])
+            cp.start()
+            c_loads.append(cp)
     pl.semaphore_wait(barrier, 2)
 
     def send(stage, idx, src, dst, dev):
@@ -319,7 +369,7 @@
         far2[i] = send(4, i, c2.at[rows, cols], x2.at[rows, cols], across)
         started.append(far2[i])
 
-    def down(g):
+    def down(g, after_first):
         for n in range(NCOL):
             cols = pl.ds(n * cols_n, cols_n)
             y = jnp.dot(abuf[...], wd[:, cols], preferred_element_type=F32).astype(BF16)
@@ -327,6 +377,8 @@
             i = g * NCOL + n
             near2[i] = send(3, i, pbuf.at[g, other, :, cols], d2.at[pl.ds(g * rows_g, rows_g), cols], partner)
             started.append(near2[i])
+            if n == 0 and after_first is not None:
+                after_first()
             if n > 0:
                 relay2(g, n - 1)
         relay2(g, NCOL - 1)
@@ -366,20 +418,21 @@
     for cp in w_loads:
         cp.wait()
     gate_up(0)
-    down(0)
-    finish1(1)
+    down(0, lambda: finish1(1))
     wait1(1)
     gate_up(1)
-    down(1)
+    down(1, None)
     finish2(0)
     wait2(0)
     finish2(1)
     wait2(1)
+    for cp in c_loads:
+        cp.wait()
     for cp in started:
         cp.wait_send()
 
 
-def mlp_call(layer, last, x, part, norm, next_norm, wg, wu, wd):
+def mlp_call(layer, last, x, part, norm, next_norm, wg, wu, wd, carry=()):
     batch, d = part.shape
     half = batch // 2
     rows_g = half // GROUPS
@@ -391,19 +444,19 @@
         own(), own(), own(), own(), own(), own(), own(),
         pltpu.VMEM((GROUPS, 2, rows_g, d), BF16), pltpu.VMEM((2 * rows_g, ff), BF16),
         pltpu.VMEM((GROUPS, 2, rows_g, d), BF16), pltpu.VMEM((GROUPS, 2, rows_g, d), BF16),
-        pltpu.SemaphoreType.DMA((3, 4)), pltpu.SemaphoreType.DMA((6, n_sem)), pltpu.SemaphoreType.DMA((6, n_sem)),
+        pltpu.SemaphoreType.DMA((3, 4)), pltpu.SemaphoreType.DMA((6, 4)), pltpu.SemaphoreType.DMA((6, n_sem)), pltpu.SemaphoreType.DMA((6, n_sem)),
     ]
-    full = jax.ShapeDtypeStruct((batch, d), BF16)
-    mine = jax.ShapeDtypeStruct((half, d), BF16)
+    full = pltpu.VMEM((batch, d), BF16)
+    mine = pltpu.VMEM((half, d), BF16)
     return pl.pallas_call(
         functools.partial(mlp_kernel, layer, last),
-        out_shape=full if last else (full, mine),
-        in_specs=[VMEM] * 4 + [ANY] * 3,
-        out_specs=VMEM if last else (VMEM, VMEM),
+        out_shape=full if last else (full, mine) + tuple(pltpu.VMEM(a.shape[1:], BF16) for a in carry),
+        in_specs=[VMEM] * 4 + [HBM] * (3 + len(carry)),
+        out_specs=VMEM if last else (VMEM,) * (2 + len(carry)),
         scratch_shapes=scratch,
-        compiler_params=pltpu.CompilerParams(collective_id=layer, has_side_effects=True, vmem_limit_bytes=48 * 2**20),
+        compiler_params=pltpu.CompilerParams(collective_id=layer, has_side_effects=True, vmem_limit_bytes=(33 if last else 33) * 2**20),
         name=f"mlp{layer}",
-    )(x, part, norm, next_norm, wg, wu, wd)
+    )(x, pltpu.with_memory_space_constraint(part, pltpu.VMEM), norm, next_norm, *in_hbm((wg, wu, wd) + tuple(carry)))
 
 
 def solution(mesh):
@@ -417,8 +470,8 @@
     def local_step(hidden, positions, k_cache, v_cache, attn_norm, w_query, w_key, w_value, w_out, mlp_norm, w_gate, w_up, w_down):
         tables = [jnp.asarray(t) for t in rope_by_position(k_cache.shape[2], k_cache.shape[4])]
         part, k_out, v_out = attention_call(0, True, positions, hidden, attn_norm, tables, w_query, w_key, w_value, w_out, k_cache, v_cache, None, None)
-        h, x_own = mlp_call(0, False, hidden, part, mlp_norm, attn_norm, w_gate, w_up, w_down)
-        part, k_out, v_out = attention_call(1, False, positions, h, None, tables, w_query, w_key, w_value, w_out, k_cache, v_cache, k_out, v_out)
+        h, x_own, *carried = mlp_call(0, False, hidden, part, mlp_norm, attn_norm, w_gate, w_up, w_down, (w_query, w_key, w_value, w_out, k_cache, v_cache))
+        part, k_out, v_out = attention_call(1, False, positions, h, None, tables, *carried, k_out, v_out)[:3]
         hidden = mlp_call(1, True, x_own, part, mlp_norm, attn_norm, w_gate, w_up, w_down)
         return hidden, k_out, v_out
 

time: 111 us -> 106 us (0.955)
  local copies, waits for them, and re-layouts: 4.39 us -> 1.01 us
    pallas_call x2, Pallas kernels: 36 us -> 31.7 us  [attention_call(): pl.pallas_call(functools.partial(attention_kernel, layer, first, chunk),...]
    unnamed x13 -> x11, local copies, waits for them, and re-layouts: 4.39 us -> 1.01 us
    pallas_call x2, Pallas kernels: 69.2 us -> 72 us  [mlp_call(): pl.pallas_call(functools.partial(mlp_kernel, layer, last), out_shape=full...]
where the time goes in v2:
time: 106 us
  Pallas kernels  104 us (98%)
    pallas_call x2, Pallas kernels, mlp_call(): pl.pallas_call(functools.partial(mlp_kernel, layer, last), out_shape=full...  72 us
    pallas_call x2, Pallas kernels, attention_call(): pl.pallas_call(functools.partial(attention_kernel, layer, first, chunk),...  31.7 us

profile of v2, /device:TPU:0, one launch (start us, length us, event | category | flops | bytes accessed | tf_op | source)
XLA Modules:
  0.0 105.5 jit_solution(17088576384459909323)
XLA Ops:
  0.6 18.6 %attention0.1 = (bf16[256,2048]{1,0:T(8,128)(2,1)S(1)}, bf16[2,256,64,2,128]{4,3,2,1,0:T(2,128)(2,1)}, bf16[2,256,64,2,128]{4,3,2,1,0:T(2,128)(2,1)}) custom-call(s32[256]{0:T(256)} %refs_0_.5, bf16[256,2048]{1,0:T(8,128)(2,1)} %x_ref.1, bf16[2,2048]{1,0:T(2,128)(2,1)} %next_norm_ref.3, f32[64,128]{1,0:T(8,128)} %constant.4.clone.refs_3_.refs_2_, ...), custom_call_target="tpu_custom_call" | custom-call | tf_op jit(solution)/shard_map/attention0/pallas_call | solution.py:251
  19.3 0.0 copy-start
  19.3 0.0 copy-start.1
  19.3 0.0 copy-start.4
  19.3 39.4 %mlp0.1 = (bf16[256,2048]{1,0:T(8,128)(2,1)S(1)}, bf16[128,2048]{1,0:T(8,128)(2,1)S(1)}, bf16[2048,512]{1,0:T(8,128)(2,1)S(1)}, bf16[2048,256]{1,0:T(8,128)(2,1)...) custom-call(bf16[256,2048]{1,0:T(8,128)(2,1)} %x_ref.1, ...), custom_call_target="tpu_custom_call" | custom-call | tf_op jit(solution)/shard_map/mlp0/pallas_call | solution.py:451
  58.7 0.0 copy-done
  58.7 0.0 copy-done.1
  58.7 0.0 copy-done.4
  58.7 0.0 copy-start.2
  58.7 0.0 copy-start.3
  58.8 13.1 %attention1.1 = (bf16[256,2048]{1,0:T(8,128)(2,1)S(1)}, bf16[2,256,64,2,128]{4,3,2,1,0:T(2,128)(2,1)}, bf16[2,256,64,2,128]{4,3,2,1,0:T(2,128)(2,1)}, bf16[256,6...) custom-call(s32[256]{0:T(256)S(1)} %copy-done.4, ...), custom_call_target="tpu_custom_call", output_to_operand_aliasing={{1}: (10, {}), {2}: (11, {}), {3}: (8, {}), {4}: (9, {})} | custom-call | tf_op jit(solution)/shard_map/attention1/pallas_call | solution.py:251
  71.9 0.0 copy-done.2
  71.9 0.0 copy-done.3
  71.9 32.7 %mlp1.1 = bf16[256,2048]{1,0:T(8,128)(2,1)S(1)} custom-call(bf16[128,2048]{1,0:T(8,128)(2,1)S(1)} %get-tuple-element.18.x_ref, bf16[256,2048]{1,0:T(8,128)(2,1)S(1)} %get-tuple-element.28.part_ref, bf16[2,2048]{1,0:T(2,128)(2,1)S(1)} %copy-done.3, bf16[2,2048]{1,0:T(2,128)(2,1)S(1)} %copy-done.2, bf16[2,2048,2048]{2,1,0:T(8,128)(2,1)} %wg_hbm.3, ...), custom_call_target="tpu_custom_call" | custom-call | tf_op jit(solution)/shard_map/mlp1/pallas_call | solution.py:451
  104.6 1.0 copy.27
Async XLA Ops:
  19.3 39.4 %copy-start = (f32[64,128]{1,0:T(8,128)S(1)}, f32[64,128]{1,0:T(8,128)}, u32[]{:S(2)}) copy-start(f32[64,128]{1,0:T(8,128)} %constant.5.clone.refs_4_.refs_3_) | copy-start | bytes 98308
  19.3 39.4 %copy-start.1 = (f32[64,128]{1,0:T(8,128)S(1)}, f32[64,128]{1,0:T(8,128)}, u32[]{:S(2)}) copy-start(f32[64,128]{1,0:T(8,128)} %constant.4.clone.refs_3_.refs_2_) | copy-start | bytes 98308
  19.3 39.4 %copy-start.4 = (s32[256]{0:T(256)S(1)}, s32[256]{0:T(256)}, u32[]{:S(2)}) copy-start(s32[256]{0:T(256)} %refs_0_.5) | copy-start | bytes 3076
  58.7 13.1 %copy-start.2 = (bf16[2,2048]{1,0:T(2,128)(2,1)S(1)}, bf16[2,2048]{1,0:T(2,128)(2,1)}, u32[]{:S(2)}) copy-start(bf16[2,2048]{1,0:T(2,128)(2,1)} %next_norm_ref.3) | copy-start | bytes 24580
  58.7 13.1 %copy-start.3 = (bf16[2,2048]{1,0:T(2,128)(2,1)S(1)}, bf16[2,2048]{1,0:T(2,128)(2,1)}, u32[]{:S(2)}) copy-start(bf16[2,2048]{1,0:T(2,128)(2,1)} %norm_ref.3) | copy-start | bytes 24580

commit v3 on v2

--- a/solution.py
+++ b/solution.py
@@ -55,12 +55,12 @@
         x_ref, wq, wk, wv, wo = x_in, wq_hbm, wk_hbm, wv_hbm, wo_hbm
         part_ref, ko_hbm, vo_hbm, kbuf, vbuf = refs[2:7]
         refs = refs[7:]
-    (cos_scr, sin_scr, lim_scr, q_scr, k_scr, v_scr, kb_scr, vb_scr, p_scr, o_scr, w_sem, in_sem, out_sem) = refs
+    (cos_scr, sin_scr, lim_scr, q_scr, k_scr, v_scr, p_scr, o_scr, w_sem, in_sem, out_sem) = refs
     batch = x_ref.shape[0]
     n_q = wq.shape[1] // 128
     n_kv = wk.shape[1] // 128
     group = n_q // n_kv
-    seq = kbuf.shape[1]
+    rows_kv = kbuf.shape[1]
     n_chunks = batch // chunk
 
     if first:
@@ -132,10 +132,7 @@
     v = jnp.dot(h, wv[...], preferred_element_type=F32)
     for j in range(n_kv):
         v_scr[pl.ds(j, batch, n_kv), :] = v[:, j * 128:(j + 1) * 128]
-    kb_scr.reshape(batch * n_kv, 128)[...] = k_scr[...].astype(BF16)
-    vb_scr.reshape(batch * n_kv, 128)[...] = v_scr[...].astype(BF16)
-
-    rows_kv = seq * n_kv
+
     kmat = kbuf.reshape(batch * rows_kv, 128)
     vmat = vbuf.reshape(batch * rows_kv, 128)
     scale = 128 ** -0.5
@@ -153,6 +150,7 @@
     lane_pair = lax.broadcasted_iota(jnp.int32, (128, 128), 1) // pair
     no_tile = jnp.zeros((128, 128), BF16)
     pairs_per_tile = 128 // pair
+    tile_row = lax.broadcasted_iota(jnp.int32, (16, 128), 0)
 
     def square(mat, base):
         top = mat[pl.ds(base, 2 * rows_kv), :]
@@ -171,14 +169,22 @@
             kv_loads[c][1].wait()
 
         def insert_body(i, carry):
-            for u in range(8):
-                b = c * chunk + i * 8 + u
-                pos = pos_ref[b]
-                kbuf[b, pos] = kb_scr[b]
-                vbuf[b, pos] = vb_scr[b]
+            writes = []
+            for u in range(16):
+                b = c * chunk + i * 16 + u
+                place = pos_ref[b] * n_kv
+                block = pl.ds(pl.multiple_of((place // 16) * 16, 16), 16)
+                here = tile_row // n_kv == (place % 16) // n_kv
+                for buf, new in ((kbuf, k_scr), (vbuf, v_scr)):
+                    rows_new = new[pl.ds(b * n_kv, 1), :]
+                    for j in range(1, n_kv):
+                        rows_new = jnp.where(tile_row % n_kv == j, new[pl.ds(b * n_kv + j, 1), :], rows_new)
+                    writes.append((buf, b, block, jnp.where(here, rows_new, buf[b, block, :].astype(F32)).astype(BF16)))
+            for buf, b, block, value in writes:
+                buf[b, block, :] = value
             return carry
 
-        lax.fori_loop(0, chunk // 8, insert_body, 0)
+        lax.fori_loop(0, chunk // 16, insert_body, 0)
 
         q_t = q_scr[pl.ds(c * cols, cols), :].T
         acc = None
@@ -219,8 +225,8 @@
 
 def attention_call(layer, first, positions, x, norm, tables, wq, wk, wv, wo, kc, vc, k_out, v_out):
     batch, d = x.shape
-    seq, n_kv, hd = kc.shape[-3:]
-    n_q = wq.shape[-1] // hd
+    hd = kc.shape[-1]
+    n_q, n_kv = wq.shape[-1] // hd, wk.shape[-1] // hd
     chunk = 64
     n_chunks = batch // chunk
     if first:
@@ -244,7 +250,6 @@
     scratch = [pltpu.VMEM(shape, BF16) for shape in big] + [
         pltpu.VMEM((batch, hd), F32), pltpu.VMEM((batch, hd), F32), pltpu.VMEM((batch * n_q // hd, hd), jnp.int32),
         pltpu.VMEM((batch * n_q, hd), F32), pltpu.VMEM((batch * n_kv, hd), F32), pltpu.VMEM((batch * n_kv, hd), F32),
-        pltpu.VMEM((batch, n_kv, hd), BF16), pltpu.VMEM((batch, n_kv, hd), BF16),
         pltpu.VMEM((chunk * n_q, hd), F32), pltpu.VMEM((batch * n_q, hd), F32),
         pltpu.SemaphoreType.DMA((5,)), pltpu.SemaphoreType.DMA((2, n_chunks)), pltpu.SemaphoreType.DMA((2, n_chunks)),
     ]
@@ -293,13 +298,6 @@
             cp = pltpu.make_async_copy(src.at[layer, pl.ds(j * n, n)], dst.at[pl.ds(j * n, n)], w_sem.at[i, j])
             cp.start()
             w_loads.append(cp)
-    c_loads = []
-    for i, (src, dst) in enumerate(zip(carry_in, carry_out)):
-        n = dst.shape[0] // 4
-        for j in range(4):
-            cp = pltpu.make_async_copy(src.at[layer + 1, pl.ds(j * n, n)], dst.at[pl.ds(j * n, n)], c_sem.at[i, j])
-            cp.start()
-            c_loads.append(cp)
     pl.semaphore_wait(barrier, 2)
 
     def send(stage, idx, src, dst, dev):
@@ -417,6 +415,13 @@
     wait1(0)
     for cp in w_loads:
         cp.wait()
+    c_loads = []
+    for i, (src, dst) in enumerate(zip(carry_in, carry_out)):
+        n = dst.shape[0] // 4
+        for j in range(4):
+            cp = pltpu.make_async_copy(src.at[layer + 1, pl.ds(j * n, n)], dst.at[pl.ds(j * n, n)], c_sem.at[i, j])
+            cp.start()
+            c_loads.append(cp)
     gate_up(0)
     down(0, lambda: finish1(1))
     wait1(1)
@@ -468,11 +473,14 @@
     split_rows = P(None, 'tp', None)
 
     def local_step(hidden, positions, k_cache, v_cache, attn_norm, w_query, w_key, w_value, w_out, mlp_norm, w_gate, w_up, w_down):
-        tables = [jnp.asarray(t) for t in rope_by_position(k_cache.shape[2], k_cache.shape[4])]
+        shape = k_cache.shape
+        flat = shape[:2] + (shape[2] * shape[3], shape[4])
+        k_cache, v_cache = k_cache.reshape(flat), v_cache.reshape(flat)
+        tables = [jnp.asarray(t) for t in rope_by_position(shape[2], shape[4])]
         part, k_out, v_out = attention_call(0, True, positions, hidden, attn_norm, tables, w_query, w_key, w_value, w_out, k_cache, v_cache, None, None)
         h, x_own, *carried = mlp_call(0, False, hidden, part, mlp_norm, attn_norm, w_gate, w_up, w_down, (w_query, w_key, w_value, w_out, k_cache, v_cache))
         part, k_out, v_out = attention_call(1, False, positions, h, None, tables, *carried, k_out, v_out)[:3]
         hidden = mlp_call(1, True, x_own, part, mlp_norm, attn_norm, w_gate, w_up, w_down)
-        return hidden, k_out, v_out
+        return hidden, k_out.reshape(shape), v_out.reshape(shape)
 
     return jax.shard_map(local_step, mesh=mesh, in_specs=(row_spec, pos_spec, cache_spec, cache_spec, norm_spec, col_spec, col_spec, col_spec, split_rows, norm_spec, col_spec, col_spec, split_rows), out_specs=(row_spec, cache_spec, cache_spec), check_vma=False)

time: 106 us -> 105 us (level)
    pallas_call x2, Pallas kernels: 72 us -> 69.6 us  [mlp_call(): pl.pallas_call(functools.partial(mlp_kernel, layer, last), out_shape=full...]
    pallas_call x2, Pallas kernels: 31.7 us -> 33.6 us  [attention_call(): pl.pallas_call(functools.partial(attention_kernel, layer, first, chunk),...]
where the time goes in v3:
time: 105 us
  Pallas kernels  103 us (98%)
    pallas_call x2, Pallas kernels, mlp_call(): pl.pallas_call(functools.partial(mlp_kernel, layer, last), out_shape=full...  69.6 us
    pallas_call x2, Pallas kernels, attention_call(): pl.pallas_call(functools.partial(attention_kernel, layer, first, chunk),...  33.6 us

profile of v3, /device:TPU:0, one launch (start us, length us, event | category | flops | bytes accessed | tf_op | source)
XLA Modules:
  0.0 104.9 jit_solution(13907707637391136735)
XLA Ops:
  0.6 19.6 %attention0.1 = (bf16[256,2048]{1,0:T(8,128)(2,1)S(1)}, bf16[2,256,128,128]{3,2,1,0:T(8,128)(2,1)}, bf16[2,256,128,128]{3,2,1,0:T(8,128)(2,1)}) custom-call(s32[256]{0:T(256)} %refs_0_.5, bf16[256,2048]{1,0:T(8,128)(2,1)} %x_ref.1, bf16[2,2048]{1,0:T(2,128)(2,1)} %next_norm_ref.3, f32[64,128]{1,0:T(8,128)} %constant.4.clone.refs_3_.refs_2_, ...), custom_call_target="tpu_custom_call" | custom-call | tf_op jit(solution)/shard_map/attention0/pallas_call | solution.py:256
  20.2 0.0 copy-start
  20.2 0.0 copy-start.1
  20.2 0.0 copy-start.4
  20.3 36.6 %mlp0.1 = (bf16[256,2048]{1,0:T(8,128)(2,1)S(1)}, bf16[128,2048]{1,0:T(8,128)(2,1)S(1)}, bf16[2048,512]{1,0:T(8,128)(2,1)S(1)}, bf16[2048,256]{1,0:T(8,128)(2,1)...) custom-call(bf16[256,2048]{1,0:T(8,128)(2,1)} %x_ref.1, ...), custom_call_target="tpu_custom_call" | custom-call | tf_op jit(solution)/shard_map/mlp0/pallas_call | solution.py:456
  56.9 0.0 copy-done
  56.9 0.0 copy-done.1
  56.9 0.0 copy-done.4
  56.9 0.0 copy-start.2
  56.9 0.0 copy-start.3
  56.9 14.0 %attention1.1 = (bf16[256,2048]{1,0:T(8,128)(2,1)S(1)}, bf16[2,256,128,128]{3,2,1,0:T(8,128)(2,1)}, bf16[2,256,128,128]{3,2,1,0:T(8,128)(2,1)}, bf16[256,128,128...) custom-call(s32[256]{0:T(256)S(1)} %copy-done.4, ...), custom_call_target="tpu_custom_call", output_to_operand_aliasing={{1}: (10, {}), {2}: (11, {}), {3}: (8, {}), {4}: (9, {})} | custom-call | tf_op jit(solution)/shard_map/attention1/pallas_call | solution.py:256
  70.9 0.0 copy-done.2
  70.9 0.0 copy-done.3
  70.9 33.0 %mlp1.1 = bf16[256,2048]{1,0:T(8,128)(2,1)S(1)} custom-call(bf16[128,2048]{1,0:T(8,128)(2,1)S(1)} %get-tuple-element.18.x_ref, bf16[256,2048]{1,0:T(8,128)(2,1)S(1)} %get-tuple-element.28.part_ref, bf16[2,2048]{1,0:T(2,128)(2,1)S(1)} %copy-done.3, bf16[2,2048]{1,0:T(2,128)(2,1)S(1)} %copy-done.2, bf16[2,2048,2048]{2,1,0:T(8,128)(2,1)} %wg_hbm.3, ...), custom_call_target="tpu_custom_call" | custom-call | tf_op jit(solution)/shard_map/mlp1/pallas_call | solution.py:456
  103.9 1.0 copy.27
Async XLA Ops:
  20.2 36.6 %copy-start = (f32[64,128]{1,0:T(8,128)S(1)}, f32[64,128]{1,0:T(8,128)}, u32[]{:S(2)}) copy-start(f32[64,128]{1,0:T(8,128)} %constant.5.clone.refs_4_.refs_3_) | copy-start | bytes 98308
  20.2 36.6 %copy-start.1 = (f32[64,128]{1,0:T(8,128)S(1)}, f32[64,128]{1,0:T(8,128)}, u32[]{:S(2)}) copy-start(f32[64,128]{1,0:T(8,128)} %constant.4.clone.refs_3_.refs_2_) | copy-start | bytes 98308
  20.2 36.6 %copy-start.4 = (s32[256]{0:T(256)S(1)}, s32[256]{0:T(256)}, u32[]{:S(2)}) copy-start(s32[256]{0:T(256)} %refs_0_.5) | copy-start | bytes 3076
  56.9 14.0 %copy-start.2 = (bf16[2,2048]{1,0:T(2,128)(2,1)S(1)}, bf16[2,2048]{1,0:T(2,128)(2,1)}, u32[]{:S(2)}) copy-start(bf16[2,2048]{1,0:T(2,128)(2,1)} %next_norm_ref.3) | copy-start | bytes 24580
  56.9 14.0 %copy-start.3 = (bf16[2,2048]{1,0:T(2,128)(2,1)S(1)}, bf16[2,2048]{1,0:T(2,128)(2,1)}, u32[]{:S(2)}) copy-start(bf16[2,2048]{1,0:T(2,128)(2,1)} %norm_ref.3) | copy-start | bytes 24580

commit v4 on v3

--- a/solution.py
+++ b/solution.py
@@ -31,9 +31,16 @@
     return np.concatenate([cos, cos], axis=1), np.concatenate([-sin, sin], axis=1)
 
 
-def rms(rows_f32, weight_f32):
-    mean_sq = jnp.mean(rows_f32 * rows_f32, axis=-1, keepdims=True)
-    return (rows_f32 * lax.rsqrt(mean_sq + 1e-5) * weight_f32).astype(BF16)
+def norm_block(read, weight, write, width):
+    step = 256
+    acc = None
+    for j in range(width // step):
+        v = read(j * step, step)
+        sq = v * v
+        acc = sq if acc is None else acc + sq
+    scale = lax.rsqrt(jnp.sum(acc, axis=-1, keepdims=True) * (1.0 / width) + 1e-5)
+    for j in range(width // step):
+        write(j * step, step, (read(j * step, step) * scale * weight(j * step, step)).astype(BF16))
 
 
 def in_hbm(arrays):
@@ -100,11 +107,13 @@
 
     if first:
         x_load.wait()
-        weight = norm_ref[layer:layer + 1, :].astype(F32)
-
         def norm_body(i, carry):
             rows = pl.ds(pl.multiple_of(i * 16, 16), 16)
-            h_scr[rows, :] = rms(x_ref[rows, :].astype(F32), weight)
+
+            def write(j, n, v):
+                h_scr[rows, j:j + n] = v
+
+            norm_block(lambda j, n: x_ref[rows, j:j + n].astype(F32), lambda j, n: norm_ref[layer:layer + 1, j:j + n].astype(F32), write, h_scr.shape[1])
             return carry
 
         lax.fori_loop(0, batch // 16, norm_body, 0)
@@ -150,7 +159,10 @@
     lane_pair = lax.broadcasted_iota(jnp.int32, (128, 128), 1) // pair
     no_tile = jnp.zeros((128, 128), BF16)
     pairs_per_tile = 128 // pair
-    tile_row = lax.broadcasted_iota(jnp.int32, (16, 128), 0)
+    per_tile = 16 // n_kv
+    shift = per_tile.bit_length() - 1
+    tile_row = lax.broadcasted_iota(jnp.int32, (16, 128), 0) // n_kv
+    tile_head = lax.broadcasted_iota(jnp.int32, (8, 128), 0) % n_kv
 
     def square(mat, base):
         top = mat[pl.ds(base, 2 * rows_kv), :]
@@ -168,23 +180,20 @@
             kv_loads[c][0].wait()
             kv_loads[c][1].wait()
 
-        def insert_body(i, carry):
+        for i in range(c * chunk, (c + 1) * chunk, 8):
             writes = []
-            for u in range(16):
-                b = c * chunk + i * 16 + u
-                place = pos_ref[b] * n_kv
-                block = pl.ds(pl.multiple_of((place // 16) * 16, 16), 16)
-                here = tile_row // n_kv == (place % 16) // n_kv
+            for b in range(i, i + 8):
+                pos = pos_ref[b]
+                block = pl.ds(pl.multiple_of(lax.shift_left(lax.shift_right_logical(pos, shift), 4), 16), 16)
+                here = tile_row == lax.bitwise_and(pos, per_tile - 1)
                 for buf, new in ((kbuf, k_scr), (vbuf, v_scr)):
-                    rows_new = new[pl.ds(b * n_kv, 1), :]
+                    fresh = jnp.broadcast_to(new[b * n_kv:b * n_kv + 1, :], (8, 128))
                     for j in range(1, n_kv):
-                        rows_new = jnp.where(tile_row % n_kv == j, new[pl.ds(b * n_kv + j, 1), :], rows_new)
-                    writes.append((buf, b, block, jnp.where(here, rows_new, buf[b, block, :].astype(F32)).astype(BF16)))
+                        fresh = jnp.where(tile_head == j, new[b * n_kv + j:b * n_kv + j + 1, :], fresh)
+                    value = jnp.where(here, jnp.concatenate([fresh, fresh], axis=0), buf[b, block, :].astype(F32))
+                    writes.append((buf, b, block, value.astype(BF16)))
             for buf, b, block, value in writes:
                 buf[b, block, :] = value
-            return carry
-
-        lax.fori_loop(0, chunk // 16, insert_body, 0)
 
         q_t = q_scr[pl.ds(c * cols, cols), :].T
         acc = None
@@ -308,6 +317,37 @@
 
     started = []
 
+    def add_norm(mine, theirs, res, res_row, row, x_to, w_ref, w_row, dst, dst_row):
+        rows = pl.ds(row, 16)
+        to = pl.ds(dst_row, 16)
+
+        def total(j, n):
+            t = (mine[rows, j:j + n].astype(F32) + theirs[rows, j:j + n].astype(F32)).astype(BF16).astype(F32)
+            return (res[pl.ds(res_row, 16), j:j + n].astype(F32) + t).astype(BF16)
+
+        if w_ref is None:
+            for j in range(0, d, 256):
+                dst[to, j:j + 256] = total(j, 256)
+            return
+
+        def keep(j, n):
+            v = total(j, n)
+            x_to[rows, j:j + n] = v
+            return v.astype(F32)
+
+        first_pass = [True] * (d // 256)
+
+        def read(j, n):
+            if first_pass[j // 256]:
+                first_pass[j // 256] = False
+                return keep(j, n)
+            return x_to[rows, j:j + n].astype(F32)
+
+        def write(j, n, v):
+            dst[to, j:j + n] = v
+
+        norm_block(read, lambda j, n: w_ref[w_row:w_row + 1, j:j + n].astype(F32), write, d)
+
     subs = [(g, s, g * rows_g + s * rows_s) for g in range(GROUPS) for s in range(SUB)]
     near = []
     for i, (g, s, r0) in enumerate(subs):
@@ -320,7 +360,6 @@
         far.append(send(1, i, c1.at[rows], x1.at[rows], across))
     started += near + far
 
-    weight = norm_ref[layer:layer + 1, :].astype(F32)
     gathers1 = {}
 
     def finish1(g):
@@ -330,11 +369,7 @@
             for r in range(rows_s // 16):
                 r0 = g * rows_g + s * rows_s + r * 16
                 rows = pl.ds(r0, 16)
-                total = (c1[rows, :].astype(F32) + x1[rows, :].astype(F32)).astype(BF16)
-                res = x_ref[pl.ds(r0, 16), :] if last else x_ref[pl.ds(core * half + r0, 16), :]
-                xn = (res.astype(F32) + total.astype(F32)).astype(BF16)
-                x_own[rows, :] = xn
-                hbuf[g, core, pl.ds(s * rows_s + r * 16, 16), :] = rms(xn.astype(F32), weight)
+                add_norm(c1, x1, x_ref, r0 if last else core * half + r0, r0, x_own, norm_ref, layer, hbuf.at[g, core], s * rows_s + r * 16)
             part = hbuf.at[g, core, pl.ds(s * rows_s, rows_s)]
             cp = send(2, i, part, part, partner)
             gathers1[i] = cp
@@ -386,19 +421,13 @@
     def finish2(g):
         for n in range(NCOL):
             far2[g * NCOL + n].wait_recv()
-        if not last:
-            nweight = next_norm_ref[layer + 1:layer + 2, :].astype(F32)
         for s in range(SUB):
             for r in range(rows_s // 16):
                 r0 = g * rows_g + s * rows_s + r * 16
-                rows = pl.ds(r0, 16)
-                total = (c2[rows, :].astype(F32) + x2[rows, :].astype(F32)).astype(BF16)
-                xn = (x_own[rows, :].astype(F32) + total.astype(F32)).astype(BF16)
                 if last:
-                    obuf[g, core, pl.ds(s * rows_s + r * 16, 16), :] = xn
+                    add_norm(c2, x2, x_own, r0, r0, None, None, 0, obuf.at[g, core], s * rows_s + r * 16)
                 else:
-                    xo_ref[rows, :] = xn
-                    obuf[g, core, pl.ds(s * rows_s + r * 16, 16), :] = rms(xn.astype(F32), nweight)
+                    add_norm(c2, x2, x_own, r0, r0, xo_ref, next_norm_ref, layer + 1, obuf.at[g, core], s * rows_s + r * 16)
             part = obuf.at[g, core, pl.ds(s * rows_s, rows_s)]
             cp = send(5, g * SUB + s, part, part, partner)
             gathers2[g * SUB + s] = cp

time: 105 us -> 98.6 us (0.939)
  Pallas kernels: 103 us -> 96.7 us
    pallas_call x2, Pallas kernels: 33.6 us -> 27.4 us  [attention_call(): pl.pallas_call(functools.partial(attention_kernel, layer, first, chunk),...]
where the time goes in v4:
time: 98.6 us; the launch traced here: 98.5 us
  Pallas kernels  96.7 us (98%)
  local copies, waits for them, and re-layouts  1.01 us (1%)
    pallas_call x2, Pallas kernels, mlp_call(): pl.pallas_call(functools.partial(mlp_kernel, layer, last), out_shape=full...  69.3 us
    pallas_call x2, Pallas kernels, attention_call(): pl.pallas_call(functools.partial(attention_kernel, layer, first, chunk),...  27.4 us

profile of v4, /device:TPU:0, one launch (start us, length us, event | category | flops | bytes accessed | tf_op | source)
XLA Modules:
  0.0 98.5 jit_solution(5237721542274122426)
XLA Ops:
  0.6 17.0 %attention0.1 = (bf16[256,2048]{1,0:T(8,128)(2,1)S(1)}, bf16[2,256,128,128]{3,2,1,0:T(8,128)(2,1)}, bf16[2,256,128,128]{3,2,1,0:T(8,128)(2,1)}) custom-call(s32[256]{0:T(256)} %refs_0_.5, bf16[256,2048]{1,0:T(8,128)(2,1)} %x_ref.1, bf16[2,2048]{1,0:T(2,128)(2,1)} %next_norm_ref.3, f32[64,128]{1,0:T(8,128)} %constant.4.clone.refs_3_.refs_2_, ...), custom_call_target="tpu_custom_call" | custom-call | tf_op jit(solution)/shard_map/attention0/pallas_call | solution.py:265
  17.6 0.0 copy-start
  17.6 0.0 copy-start.1
  17.6 0.0 copy-start.4
  17.7 36.6 %mlp0.1 = (bf16[256,2048]{1,0:T(8,128)(2,1)S(1)}, bf16[128,2048]{1,0:T(8,128)(2,1)S(1)}, bf16[2048,512]{1,0:T(8,128)(2,1)S(1)}, bf16[2048,256]{1,0:T(8,128)(2,1)...) custom-call(bf16[256,2048]{1,0:T(8,128)(2,1)} %x_ref.1, ...), custom_call_target="tpu_custom_call" | custom-call | tf_op jit(solution)/shard_map/mlp0/pallas_call | solution.py:485
  54.2 0.0 copy-done
  54.3 0.0 copy-done.1
  54.3 0.0 copy-done.4
  54.3 0.0 copy-start.2
  54.3 0.0 copy-start.3
  54.3 10.4 %attention1.1 = (bf16[256,2048]{1,0:T(8,128)(2,1)S(1)}, bf16[2,256,128,128]{3,2,1,0:T(8,128)(2,1)}, bf16[2,256,128,128]{3,2,1,0:T(8,128)(2,1)}, bf16[256,128,128...) custom-call(s32[256]{0:T(256)S(1)} %copy-done.4, ...), custom_call_target="tpu_custom_call", output_to_operand_aliasing={{1}: (10, {}), {2}: (11, {}), {3}: (8, {}), {4}: (9, {})} | custom-call | tf_op jit(solution)/shard_map/attention1/pallas_call | solution.py:265
  64.7 0.0 copy-done.2
  64.7 0.0 copy-done.3
  64.7 32.8 %mlp1.1 = bf16[256,2048]{1,0:T(8,128)(2,1)S(1)} custom-call(bf16[128,2048]{1,0:T(8,128)(2,1)S(1)} %get-tuple-element.18.x_ref, bf16[256,2048]{1,0:T(8,128)(2,1)S(1)} %get-tuple-element.28.part_ref, bf16[2,2048]{1,0:T(2,128)(2,1)S(1)} %copy-done.3, bf16[2,2048]{1,0:T(2,128)(2,1)S(1)} %copy-done.2, bf16[2,2048,2048]{2,1,0:T(8,128)(2,1)} %wg_hbm.3, ...), custom_call_target="tpu_custom_call" | custom-call | tf_op jit(solution)/shard_map/mlp1/pallas_call | solution.py:485
  97.5 1.0 copy.27
Async XLA Ops:
  17.6 36.6 %copy-start = (f32[64,128]{1,0:T(8,128)S(1)}, f32[64,128]{1,0:T(8,128)}, u32[]{:S(2)}) copy-start(f32[64,128]{1,0:T(8,128)} %constant.5.clone.refs_4_.refs_3_) | copy-start | bytes 98308
  17.6 36.6 %copy-start.1 = (f32[64,128]{1,0:T(8,128)S(1)}, f32[64,128]{1,0:T(8,128)}, u32[]{:S(2)}) copy-start(f32[64,128]{1,0:T(8,128)} %constant.4.clone.refs_3_.refs_2_) | copy-start | bytes 98308
  17.6 36.6 %copy-start.4 = (s32[256]{0:T(256)S(1)}, s32[256]{0:T(256)}, u32[]{:S(2)}) copy-start(s32[256]{0:T(256)} %refs_0_.5) | copy-start | bytes 3076
  54.3 10.4 %copy-start.2 = (bf16[2,2048]{1,0:T(2,128)(2,1)S(1)}, bf16[2,2048]{1,0:T(2,128)(2,1)}, u32[]{:S(2)}) copy-start(bf16[2,2048]{1,0:T(2,128)(2,1)} %next_norm_ref.3) | copy-start | bytes 24580
  54.3 10.4 %copy-start.3 = (bf16[2,2048]{1,0:T(2,128)(2,1)S(1)}, bf16[2,2048]{1,0:T(2,128)(2,1)}, u32[]{:S(2)}) copy-start(bf16[2,2048]{1,0:T(2,128)(2,1)} %norm_ref.3) | copy-start | bytes 24580

commit v5 on v4

--- a/solution.py
+++ b/solution.py
@@ -175,6 +175,14 @@
         stores.append((pltpu.make_async_copy(kbuf.at[rows], ko_hbm.at[layer, rows], out_sem.at[0, c]),
                        pltpu.make_async_copy(vbuf.at[rows], vo_hbm.at[layer, rows], out_sem.at[1, c])))
 
+    def values(c):
+        for t in range(quads):
+            b = c * chunk + t * 4
+            p4 = p_scr[c % 2, pl.ds(t * 2 * pair, 2 * pair), :]
+            wide = jnp.concatenate([jnp.where(first_in_pair, p4, zero), jnp.where(first_in_pair, zero, p4)], axis=1).astype(BF16)
+            o = jnp.dot(wide, square(vmat, b * rows_kv), preferred_element_type=F32)
+            o_scr[pl.ds(b * n_q, 2 * pair), :] = jnp.where(first_pair, o[:, :128], o[:, 128:])
+
     for c in range(n_chunks):
         if first:
             kv_loads[c][0].wait()
@@ -207,19 +215,16 @@
                 halves.append(jnp.concatenate(tiles, axis=1))
             d = jnp.dot(square(kmat, (c * chunk + t * 4) * rows_kv), jnp.concatenate(halves, axis=0), preferred_element_type=F32)
             acc = d if acc is None else acc + d
+        if c > 0:
+            values(c - 1)
         stores[c][0].start()
         stores[c][1].start()
         s = jnp.where(first_of_two, acc[:rows_kv], acc[rows_kv:])
         limit = jnp.concatenate([lim_scr[pl.ds(c * (cols // 128) + j, 1), :] for j in range(cols // 128)], axis=1)
         s = jnp.where(same_head & (row <= limit), s * scale, -jnp.inf)
         e = jnp.exp(s - jnp.max(s, axis=0, keepdims=True))
-        p_scr[...] = (e * (1.0 / jnp.sum(e, axis=0, keepdims=True))).T
-        for t in range(quads):
-            b = c * chunk + t * 4
-            p4 = p_scr[pl.ds(t * 2 * pair, 2 * pair), :]
-            wide = jnp.concatenate([jnp.where(first_in_pair, p4, zero), jnp.where(first_in_pair, zero, p4)], axis=1).astype(BF16)
-            o = jnp.dot(wide, square(vmat, b * rows_kv), preferred_element_type=F32)
-            o_scr[pl.ds(b * n_q, 2 * pair), :] = jnp.where(first_pair, o[:, :128], o[:, 128:])
+        p_scr[c % 2] = (e * (1.0 / jnp.sum(e, axis=0, keepdims=True))).T
+    values(n_chunks - 1)
 
     att = jnp.concatenate([o_scr[pl.ds(j, batch, n_q), :].astype(BF16) for j in range(n_q)], axis=1)
     if first:
@@ -259,7 +264,7 @@
     scratch = [pltpu.VMEM(shape, BF16) for shape in big] + [
         pltpu.VMEM((batch, hd), F32), pltpu.VMEM((batch, hd), F32), pltpu.VMEM((batch * n_q // hd, hd), jnp.int32),
         pltpu.VMEM((batch * n_q, hd), F32), pltpu.VMEM((batch * n_kv, hd), F32), pltpu.VMEM((batch * n_kv, hd), F32),
-        pltpu.VMEM((chunk * n_q, hd), F32), pltpu.VMEM((batch * n_q, hd), F32),
+        pltpu.VMEM((2, chunk * n_q, hd), F32), pltpu.VMEM((batch * n_q, hd), F32),
         pltpu.SemaphoreType.DMA((5,)), pltpu.SemaphoreType.DMA((2, n_chunks)), pltpu.SemaphoreType.DMA((2, n_chunks)),
     ]
     return pl.pallas_call(

time: 98.6 us -> 94.5 us (0.958)
  Pallas kernels: 96.7 us -> 92.6 us
    pallas_call x2, Pallas kernels: 27.4 us -> 23.2 us  [attention_call(): pl.pallas_call(functools.partial(attention_kernel, layer, first, chunk),...]
where the time goes in v5:
time: 94.5 us; the launch traced here: 94.3 us
  Pallas kernels  92.6 us (98%)
  local copies, waits for them, and re-layouts  1.01 us (1%)
    pallas_call x2, Pallas kernels, mlp_call(): pl.pallas_call(functools.partial(mlp_kernel, layer, last), out_shape=full...  69.3 us
    pallas_call x2, Pallas kernels, attention_call(): pl.pallas_call(functools.partial(attention_kernel, layer, first, chunk),...  23.2 us

profile of v5, /device:TPU:0, one launch (start us, length us, event | category | flops | bytes accessed | tf_op | source)
XLA Modules:
  0.0 94.3 jit_solution(7867851812954350443)
XLA Ops:
  0.6 14.6 %attention0.1 = (bf16[256,2048]{1,0:T(8,128)(2,1)S(1)}, bf16[2,256,128,128]{3,2,1,0:T(8,128)(2,1)}, bf16[2,256,128,128]{3,2,1,0:T(8,128)(2,1)}) custom-call(s32[256]{0:T(256)} %refs_0_.5, bf16[256,2048]{1,0:T(8,128)(2,1)} %x_ref.1, bf16[2,2048]{1,0:T(2,128)(2,1)} %next_norm_ref.3, f32[64,128]{1,0:T(8,128)} %constant.4.clone.refs_3_.refs_2_, ...), custom_call_target="tpu_custom_call" | custom-call | tf_op jit(solution)/shard_map/attention0/pallas_call | solution.py:270
  15.3 0.0 copy-start
  15.3 0.0 copy-start.1
  15.3 0.0 copy-start.4
  15.3 36.6 %mlp0.1 = (bf16[256,2048]{1,0:T(8,128)(2,1)S(1)}, bf16[128,2048]{1,0:T(8,128)(2,1)S(1)}, bf16[2048,512]{1,0:T(8,128)(2,1)S(1)}, bf16[2048,256]{1,0:T(8,128)(2,1)...) custom-call(bf16[256,2048]{1,0:T(8,128)(2,1)} %x_ref.1, ...), custom_call_target="tpu_custom_call" | custom-call | tf_op jit(solution)/shard_map/mlp0/pallas_call | solution.py:490
  51.9 0.0 copy-done
  51.9 0.0 copy-done.1
  51.9 0.0 copy-done.4
  51.9 0.0 copy-start.2
  51.9 0.0 copy-start.3
  51.9 8.6 %attention1.1 = (bf16[256,2048]{1,0:T(8,128)(2,1)S(1)}, bf16[2,256,128,128]{3,2,1,0:T(8,128)(2,1)}, bf16[2,256,128,128]{3,2,1,0:T(8,128)(2,1)}, bf16[256,128,128...) custom-call(s32[256]{0:T(256)S(1)} %copy-done.4, ...), custom_call_target="tpu_custom_call", output_to_operand_aliasing={{1}: (10, {}), {2}: (11, {}), {3}: (8, {}), {4}: (9, {})} | custom-call | tf_op jit(solution)/shard_map/attention1/pallas_call | solution.py:270
  60.6 0.0 copy-done.2
  60.6 0.0 copy-done.3
  60.6 32.7 %mlp1.1 = bf16[256,2048]{1,0:T(8,128)(2,1)S(1)} custom-call(bf16[128,2048]{1,0:T(8,128)(2,1)S(1)} %get-tuple-element.18.x_ref, bf16[256,2048]{1,0:T(8,128)(2,1)S(1)} %get-tuple-element.28.part_ref, bf16[2,2048]{1,0:T(2,128)(2,1)S(1)} %copy-done.3, bf16[2,2048]{1,0:T(2,128)(2,1)S(1)} %copy-done.2, bf16[2,2048,2048]{2,1,0:T(8,128)(2,1)} %wg_hbm.3, ...), custom_call_target="tpu_custom_call" | custom-call | tf_op jit(solution)/shard_map/mlp1/pallas_call | solution.py:490
  93.3 1.0 %copy.27 = bf16[256,2048]{1,0:T(8,128)(2,1)} copy(bf16[256,2048]{1,0:T(8,128)(2,1)S(1)} %mlp1.1) | data formatting | bytes 2097152
Async XLA Ops:
  15.3 36.6 %copy-start = (f32[64,128]{1,0:T(8,128)S(1)}, f32[64,128]{1,0:T(8,128)}, u32[]{:S(2)}) copy-start(f32[64,128]{1,0:T(8,128)} %constant.5.clone.refs_4_.refs_3_) | copy-start | bytes 98308
  15.3 36.6 %copy-start.1 = (f32[64,128]{1,0:T(8,128)S(1)}, f32[64,128]{1,0:T(8,128)}, u32[]{:S(2)}) copy-start(f32[64,128]{1,0:T(8,128)} %constant.4.clone.refs_3_.refs_2_) | copy-start | bytes 98308
  15.3 36.6 %copy-start.4 = (s32[256]{0:T(256)S(1)}, s32[256]{0:T(256)}, u32[]{:S(2)}) copy-start(s32[256]{0:T(256)} %refs_0_.5) | copy-start | bytes 3076
  51.9 8.6 %copy-start.2 = (bf16[2,2048]{1,0:T(2,128)(2,1)S(1)}, bf16[2,2048]{1,0:T(2,128)(2,1)}, u32[]{:S(2)}) copy-start(bf16[2,2048]{1,0:T(2,128)(2,1)} %next_norm_ref.3) | copy-start | bytes 24580
  51.9 8.6 %copy-start.3 = (bf16[2,2048]{1,0:T(2,128)(2,1)S(1)}, bf16[2,2048]{1,0:T(2,128)(2,1)}, u32[]{:S(2)}) copy-start(bf16[2,2048]{1,0:T(2,128)(2,1)} %norm_ref.3) | copy-start | bytes 24580

commit v6 on v5

--- a/solution.py
+++ b/solution.py
@@ -51,13 +51,18 @@
     refs = list(refs)
     pos_ref = refs.pop(0)
     x_in = refs.pop(0)
-    norm_ref = refs.pop(0) if first else None
+    norm_in = refs.pop(0) if first else None
     cos_tab, sin_tab, wq_hbm, wk_hbm, wv_hbm, wo_hbm, kc_hbm, vc_hbm = refs[:8]
     refs = refs[8:]
     if first:
         part_ref, ko_hbm, vo_hbm = refs[:3]
-        x_ref, wq, wk, wv, wo, kbuf, vbuf, h_scr = refs[3:11]
-        refs = refs[11:]
+        x_ref, wq, wk, wv, wo, kbuf, vbuf, h_scr, norm_ref, cos_ref, sin_ref, pos_smem, small_sem = refs[3:16]
+        refs = refs[16:]
+        small = []
+        for i, (src, dst) in enumerate(((pos_ref, pos_smem), (cos_tab, cos_ref), (sin_tab, sin_ref), (norm_in, norm_ref))):
+            small.append(pltpu.make_async_copy(src, dst, small_sem.at[i]))
+            small[i].start()
+        pos_ref, cos_tab, sin_tab = pos_smem, cos_ref, sin_ref
     else:
         x_ref, wq, wk, wv, wo = x_in, wq_hbm, wk_hbm, wv_hbm, wo_hbm
         part_ref, ko_hbm, vo_hbm, kbuf, vbuf = refs[2:7]
@@ -88,6 +93,10 @@
             kv_loads.append((a, b))
         wo_load = pltpu.make_async_copy(wo_hbm.at[layer], wo, w_sem.at[3])
         wo_load.start()
+
+    if first:
+        for cp in small:
+            cp.wait()
 
     per_row = 128 // n_q
     lane_request = lax.broadcasted_iota(jnp.int32, (1, 128), 1) // n_q
@@ -244,12 +253,12 @@
     chunk = 64
     n_chunks = batch // chunk
     if first:
-        ins = [positions] + in_hbm([x]) + [norm, tables[0], tables[1]] + in_hbm([wq, wk, wv, wo, kc, vc])
+        ins = in_hbm([positions, x, norm, tables[0], tables[1], wq, wk, wv, wo, kc, vc])
     else:
         ins = [positions, x, tables[0], tables[1], wq, wk, wv, wo, kc, vc]
     part = pltpu.VMEM((batch, d), BF16)
     if first:
-        specs = [SMEM, HBM, VMEM, VMEM, VMEM] + [HBM] * 6
+        specs = [HBM] * 11
         outs = (part, pltpu.HBM(kc.shape, BF16), pltpu.HBM(vc.shape, BF16))
         out_specs = (VMEM, HBM, HBM)
         aliases = {}
@@ -261,7 +270,11 @@
         ins += in_hbm([k_out, v_out])
         out_specs = (VMEM, HBM, HBM, VMEM, VMEM)
         big = []
-    scratch = [pltpu.VMEM(shape, BF16) for shape in big] + [
+    scratch = [pltpu.VMEM(shape, BF16) for shape in big]
+    if first:
+        scratch += [pltpu.VMEM(norm.shape, BF16), pltpu.VMEM(tables[0].shape, F32), pltpu.VMEM(tables[1].shape, F32),
+                    pltpu.SMEM((batch,), jnp.int32), pltpu.SemaphoreType.DMA((4,))]
+    scratch += [
         pltpu.VMEM((batch, hd), F32), pltpu.VMEM((batch, hd), F32), pltpu.VMEM((batch * n_q // hd, hd), jnp.int32),
         pltpu.VMEM((batch * n_q, hd), F32), pltpu.VMEM((batch * n_kv, hd), F32), pltpu.VMEM((batch * n_kv, hd), F32),
         pltpu.VMEM((2, chunk * n_q, hd), F32), pltpu.VMEM((batch * n_q, hd), F32),
@@ -284,19 +297,20 @@
 NCOL = 4
 
 
-def mlp_kernel(layer, last, x_ref, part_ref, norm_ref, next_norm_ref, wg_hbm, wu_hbm, wd_hbm, *refs):
+def mlp_kernel(layer, last, x_in, part_ref, norm_in, next_norm_in, wg_hbm, wu_hbm, wd_hbm, *refs):
     if last:
         carry_in, carry_out = (), ()
         (xo_ref,), refs = refs[:1], refs[1:]
     else:
         carry_in, (ho_ref, xo_ref), carry_out, refs = refs[:6], refs[6:8], refs[8:14], refs[14:]
-    (wg, wu, wd, d1, c1, x1, d2, c2, x2, x_own, hbuf, abuf, pbuf, obuf, w_sem, c_sem, s_send, s_recv) = refs
+    (wg, wu, wd, d1, c1, x1, d2, c2, x2, x_own, hbuf, abuf, pbuf, norm_ref, next_norm_ref, n_sem, w_sem, c_sem, s_send, s_recv) = refs
     t = lax.axis_index("tp")
     core = lax.rem(t, 2)
     other = 1 - core
     partner = t + other - core
     across = lax.rem(t + 2, 4)
-    d = x_ref.shape[1]
+    out = xo_ref if last else ho_ref
+    d = part_ref.shape[1]
     half = d1.shape[0]
     rows_g = half // GROUPS
     rows_s = rows_g // SUB
@@ -305,6 +319,11 @@
     barrier = pltpu.get_barrier_semaphore()
     for dev in (partner, across):
         pl.semaphore_signal(barrier, inc=1, device_id={"tp": dev}, device_id_type=MESH)
+    small = [pltpu.make_async_copy(norm_in, norm_ref, n_sem.at[0]), pltpu.make_async_copy(next_norm_in, next_norm_ref, n_sem.at[1])]
+    if not last:
+        small.append(pltpu.make_async_copy(x_in.at[pl.ds(pl.multiple_of(core * half, half), half)], x_own, n_sem.at[2]))
+    for cp in small:
+        cp.start()
     w_loads = []
     for i, (src, dst) in enumerate(((wg_hbm, wg), (wu_hbm, wu), (wd_hbm, wd))):
         n = dst.shape[0] // 4
@@ -374,7 +393,7 @@
             for r in range(rows_s // 16):
                 r0 = g * rows_g + s * rows_s + r * 16
                 rows = pl.ds(r0, 16)
-                add_norm(c1, x1, x_ref, r0 if last else core * half + r0, r0, x_own, norm_ref, layer, hbuf.at[g, core], s * rows_s + r * 16)
+                add_norm(c1, x1, x_in if last else x_own, r0, r0, x_own, norm_ref, layer, hbuf.at[g, core], s * rows_s + r * 16)
             part = hbuf.at[g, core, pl.ds(s * rows_s, rows_s)]
             cp = send(2, i, part, part, partner)
             gathers1[i] = cp
@@ -388,13 +407,14 @@
         hid = hbuf.at[g].reshape(2 * rows_g, d)
 
         def body(n, carry):
-            cols = pl.ds(pl.multiple_of(n * 512, 512), 512)
+            cols = pl.ds(n * 512, 512)
             gate = jnp.dot(hid[...], wg[:, cols], preferred_element_type=F32).astype(BF16).astype(F32)
             up = jnp.dot(hid[...], wu[:, cols], preferred_element_type=F32).astype(BF16).astype(F32)
             abuf[:, cols] = (gate * (1.0 / (1.0 + jnp.exp(-gate))) * up).astype(BF16)
             return carry
 
-        lax.fori_loop(0, wg.shape[1] // 512, body, 0)
+        for n in range(wg.shape[1] // 512):
+            body(n, 0)
 
     near2, far2 = {}, {}
 
@@ -429,22 +449,22 @@
         for s in range(SUB):
             for r in range(rows_s // 16):
                 r0 = g * rows_g + s * rows_s + r * 16
+                to = pl.multiple_of(core * half + r0, 16)
                 if last:
-                    add_norm(c2, x2, x_own, r0, r0, None, None, 0, obuf.at[g, core], s * rows_s + r * 16)
+                    add_norm(c2, x2, x_own, r0, r0, None, None, 0, out, to)
                 else:
-                    add_norm(c2, x2, x_own, r0, r0, xo_ref, next_norm_ref, layer + 1, obuf.at[g, core], s * rows_s + r * 16)
-            part = obuf.at[g, core, pl.ds(s * rows_s, rows_s)]
+                    add_norm(c2, x2, x_own, r0, r0, xo_ref, next_norm_ref, layer + 1, out, to)
+            part = out.at[pl.ds(pl.multiple_of(core * half + g * rows_g + s * rows_s, rows_s), rows_s)]
             cp = send(5, g * SUB + s, part, part, partner)
             gathers2[g * SUB + s] = cp
             started.append(cp)
 
     def wait2(g):
-        out = xo_ref if last else ho_ref
         for s in range(SUB):
             gathers2[g * SUB + s].wait_recv()
-        for c in range(2):
-            out[c * half + g * rows_g:c * half + (g + 1) * rows_g, :] = obuf[g, c]
-
+
+    for cp in small:
+        cp.wait()
     finish1(0)
     wait1(0)
     for cp in w_loads:
@@ -482,20 +502,21 @@
         pltpu.VMEM(wg.shape[1:], BF16), pltpu.VMEM(wu.shape[1:], BF16), pltpu.VMEM(wd.shape[1:], BF16),
         own(), own(), own(), own(), own(), own(), own(),
         pltpu.VMEM((GROUPS, 2, rows_g, d), BF16), pltpu.VMEM((2 * rows_g, ff), BF16),
-        pltpu.VMEM((GROUPS, 2, rows_g, d), BF16), pltpu.VMEM((GROUPS, 2, rows_g, d), BF16),
-        pltpu.SemaphoreType.DMA((3, 4)), pltpu.SemaphoreType.DMA((6, 4)), pltpu.SemaphoreType.DMA((6, n_sem)), pltpu.SemaphoreType.DMA((6, n_sem)),
+        pltpu.VMEM((GROUPS, 2, rows_g, d), BF16), pltpu.VMEM(norm.shape, BF16), pltpu.VMEM(norm.shape, BF16),
+        pltpu.SemaphoreType.DMA((3,)), pltpu.SemaphoreType.DMA((3, 4)), pltpu.SemaphoreType.DMA((6, 4)), pltpu.SemaphoreType.DMA((6, n_sem)), pltpu.SemaphoreType.DMA((6, n_sem)),
     ]
     full = pltpu.VMEM((batch, d), BF16)
     mine = pltpu.VMEM((half, d), BF16)
     return pl.pallas_call(
         functools.partial(mlp_kernel, layer, last),
         out_shape=full if last else (full, mine) + tuple(pltpu.VMEM(a.shape[1:], BF16) for a in carry),
-        in_specs=[VMEM] * 4 + [HBM] * (3 + len(carry)),
+        in_specs=[VMEM if last else HBM, VMEM] + [HBM] * (5 + len(carry)),
         out_specs=VMEM if last else (VMEM,) * (2 + len(carry)),
         scratch_shapes=scratch,
         compiler_params=pltpu.CompilerParams(collective_id=layer, has_side_effects=True, vmem_limit_bytes=(33 if last else 33) * 2**20),
         name=f"mlp{layer}",
-    )(x, pltpu.with_memory_space_constraint(part, pltpu.VMEM), norm, next_norm, *in_hbm((wg, wu, wd) + tuple(carry)))
+    )(pltpu.with_memory_space_constraint(x, pltpu.VMEM if last else pltpu.HBM), pltpu.with_memory_space_constraint(part, pltpu.VMEM),
+      *in_hbm((norm, next_norm, wg, wu, wd) + tuple(carry)))
 
 
 def solution(mesh):

time: 94.5 us -> 95.2 us (level)
    pallas_call x2, Pallas kernels: 23.2 us -> 26.5 us  [attention_call(): pl.pallas_call(functools.partial(attention_kernel, layer, first, chunk),...]
    pallas_call x2, Pallas kernels: 69.3 us -> 66.8 us  [mlp_call(): pl.pallas_call(functools.partial(mlp_kernel, layer, last), out_shape=full...]
where the time goes in v6:
time: 95.2 us; the launch traced here: 95 us
  Pallas kernels  93.3 us (98%)
  local copies, waits for them, and re-layouts  0.99 us (1%)
    pallas_call x2, Pallas kernels, mlp_call(): pl.pallas_call(functools.partial(mlp_kernel, layer, last), out_shape=full...  66.8 us
    pallas_call x2, Pallas kernels, attention_call(): pl.pallas_call(functools.partial(attention_kernel, layer, first, chunk),...  26.5 us

profile of v6, /device:TPU:0, one launch (start us, length us, event | category | flops | bytes accessed | tf_op | source)
XLA Modules:
  0.0 95.0 jit_solution(344541393695775549)
XLA Ops:
  0.6 17.9 %attention0.1 = (bf16[256,2048]{1,0:T(8,128)(2,1)S(1)}, bf16[2,256,128,128]{3,2,1,0:T(8,128)(2,1)}, bf16[2,256,128,128]{3,2,1,0:T(8,128)(2,1)}) custom-call(s32[256]{0:T(256)} %refs_0_.5, bf16[256,2048]{1,0:T(8,128)(2,1)} %x_in.1, bf16[2,2048]{1,0:T(2,128)(2,1)} %next_norm_in.3, f32[64,128]{1,0:T(8,128)} %constant.4.clone.refs_3_.refs_2_, ...), custom_call_target="tpu_custom_call" | custom-call | tf_op jit(solution)/shard_map/attention0/pallas_call | solution.py:283
  18.6 0.0 copy-start
  18.6 0.0 copy-start.1
  18.6 0.0 copy-start.2
  18.6 34.7 %mlp0.1 = (bf16[256,2048]{1,0:T(8,128)(2,1)S(1)}, bf16[128,2048]{1,0:T(8,128)(2,1)S(1)}, bf16[2048,512]{1,0:T(8,128)(2,1)S(1)}, bf16[2048,256]{1,0:T(8,128)(2,1)...) custom-call(bf16[256,2048]{1,0:T(8,128)(2,1)} %x_in.1, ...), custom_call_target="tpu_custom_call" | custom-call | tf_op jit(solution)/shard_map/mlp0/pallas_call | solution.py:510
  53.4 0.0 copy-done
  53.4 0.0 copy-done.1
  53.4 0.0 copy-done.2
  53.4 8.6 %attention1.1 = (bf16[256,2048]{1,0:T(8,128)(2,1)S(1)}, bf16[2,256,128,128]{3,2,1,0:T(8,128)(2,1)}, bf16[2,256,128,128]{3,2,1,0:T(8,128)(2,1)}, bf16[256,128,128...) custom-call(s32[256]{0:T(256)S(1)} %copy-done.2, ...), custom_call_target="tpu_custom_call", output_to_operand_aliasing={{1}: (10, {}), {2}: (11, {}), {3}: (8, {}), {4}: (9, {})} | custom-call | tf_op jit(solution)/shard_map/attention1/pallas_call | solution.py:283
  62.0 32.0 %mlp1.1 = bf16[256,2048]{1,0:T(8,128)(2,1)S(1)} custom-call(bf16[128,2048]{1,0:T(8,128)(2,1)S(1)} %get-tuple-element.18.x_in, bf16[256,2048]{1,0:T(8,128)(2,1)S(1)} %get-tuple-element.28.part_ref, bf16[2,2048]{1,0:T(2,128)(2,1)} %norm_in.3, bf16[2,2048]{1,0:T(2,128)(2,1)} %next_norm_in.3, bf16[2,2048,2048]{2,1,0:T(8,128)(2,1)} %wg_hbm.3, ...), custom_call_target="tpu_custom_call" | custom-call | tf_op jit(solution)/shard_map/mlp1/pallas_call | solution.py:510
  94.1 1.0 %copy.27 = bf16[256,2048]{1,0:T(8,128)(2,1)} copy(bf16[256,2048]{1,0:T(8,128)(2,1)S(1)} %mlp1.1) | data formatting | bytes 2097152
Async XLA Ops:
  18.6 34.8 %copy-start = (f32[64,128]{1,0:T(8,128)S(1)}, f32[64,128]{1,0:T(8,128)}, u32[]{:S(2)}) copy-start(f32[64,128]{1,0:T(8,128)} %constant.5.clone.refs_4_.refs_3_) | copy-start | bytes 98308
  18.6 34.8 %copy-start.1 = (f32[64,128]{1,0:T(8,128)S(1)}, f32[64,128]{1,0:T(8,128)}, u32[]{:S(2)}) copy-start(f32[64,128]{1,0:T(8,128)} %constant.4.clone.refs_3_.refs_2_) | copy-start | bytes 98308
  18.6 34.8 %copy-start.2 = (s32[256]{0:T(256)S(1)}, s32[256]{0:T(256)}, u32[]{:S(2)}) copy-start(s32[256]{0:T(256)} %refs_0_.5) | copy-start | bytes 3076

commit v7 on v6

--- a/solution.py
+++ b/solution.py
@@ -51,18 +51,13 @@
     refs = list(refs)
     pos_ref = refs.pop(0)
     x_in = refs.pop(0)
-    norm_in = refs.pop(0) if first else None
+    norm_ref = refs.pop(0) if first else None
     cos_tab, sin_tab, wq_hbm, wk_hbm, wv_hbm, wo_hbm, kc_hbm, vc_hbm = refs[:8]
     refs = refs[8:]
     if first:
         part_ref, ko_hbm, vo_hbm = refs[:3]
-        x_ref, wq, wk, wv, wo, kbuf, vbuf, h_scr, norm_ref, cos_ref, sin_ref, pos_smem, small_sem = refs[3:16]
-        refs = refs[16:]
-        small = []
-        for i, (src, dst) in enumerate(((pos_ref, pos_smem), (cos_tab, cos_ref), (sin_tab, sin_ref), (norm_in, norm_ref))):
-            small.append(pltpu.make_async_copy(src, dst, small_sem.at[i]))
-            small[i].start()
-        pos_ref, cos_tab, sin_tab = pos_smem, cos_ref, sin_ref
+        x_ref, wq, wk, wv, wo, kbuf, vbuf, h_scr = refs[3:11]
+        refs = refs[11:]
     else:
         x_ref, wq, wk, wv, wo = x_in, wq_hbm, wk_hbm, wv_hbm, wo_hbm
         part_ref, ko_hbm, vo_hbm, kbuf, vbuf = refs[2:7]
@@ -88,15 +83,10 @@
             rows = pl.ds(c * chunk, chunk)
             a = pltpu.make_async_copy(kc_hbm.at[layer, rows], kbuf.at[rows], in_sem.at[0, c])
             b = pltpu.make_async_copy(vc_hbm.at[layer, rows], vbuf.at[rows], in_sem.at[1, c])
-            a.start()
-            b.start()
             kv_loads.append((a, b))
         wo_load = pltpu.make_async_copy(wo_hbm.at[layer], wo, w_sem.at[3])
-        wo_load.start()
-
-    if first:
-        for cp in small:
-            cp.wait()
+        kv_loads[0][0].start()
+        kv_loads[0][1].start()
 
     per_row = 128 // n_q
     lane_request = lax.broadcasted_iota(jnp.int32, (1, 128), 1) // n_q
@@ -137,16 +127,23 @@
     h = h_src[...]
     if first:
         loads[0].wait()
+        kv_loads[1][0].start()
+        kv_loads[1][1].start()
     q = jnp.dot(h, wq[...], preferred_element_type=F32)
     for j in range(n_q):
         q_scr[pl.ds(j, batch, n_q), :] = rope(q[:, j * 128:(j + 1) * 128])
     if first:
         loads[1].wait()
+        kv_loads[2][0].start()
+        kv_loads[2][1].start()
     k = jnp.dot(h, wk[...], preferred_element_type=F32)
     for j in range(n_kv):
         k_scr[pl.ds(j, batch, n_kv), :] = rope(k[:, j * 128:(j + 1) * 128])
     if first:
         loads[2].wait()
+        kv_loads[3][0].start()
+        kv_loads[3][1].start()
+        wo_load.start()
     v = jnp.dot(h, wv[...], preferred_element_type=F32)
     for j in range(n_kv):
         v_scr[pl.ds(j, batch, n_kv), :] = v[:, j * 128:(j + 1) * 128]
@@ -253,12 +250,12 @@
     chunk = 64
     n_chunks = batch // chunk
     if first:
-        ins = in_hbm([positions, x, norm, tables[0], tables[1], wq, wk, wv, wo, kc, vc])
+        ins = [positions] + in_hbm([x]) + [norm, tables[0], tables[1]] + in_hbm([wq, wk, wv, wo, kc, vc])
     else:
         ins = [positions, x, tables[0], tables[1], wq, wk, wv, wo, kc, vc]
     part = pltpu.VMEM((batch, d), BF16)
     if first:
-        specs = [HBM] * 11
+        specs = [SMEM, HBM, VMEM, VMEM, VMEM] + [HBM] * 6
         outs = (part, pltpu.HBM(kc.shape, BF16), pltpu.HBM(vc.shape, BF16))
         out_specs = (VMEM, HBM, HBM)
         aliases = {}
@@ -271,9 +268,6 @@
         out_specs = (VMEM, HBM, HBM, VMEM, VMEM)
         big = []
     scratch = [pltpu.VMEM(shape, BF16) for shape in big]
-    if first:
-        scratch += [pltpu.VMEM(norm.shape, BF16), pltpu.VMEM(tables[0].shape, F32), pltpu.VMEM(tables[1].shape, F32),
-                    pltpu.SMEM((batch,), jnp.int32), pltpu.SemaphoreType.DMA((4,))]
     scratch += [
         pltpu.VMEM((batch, hd), F32), pltpu.VMEM((batch, hd), F32), pltpu.VMEM((batch * n_q // hd, hd), jnp.int32),
         pltpu.VMEM((batch * n_q, hd), F32), pltpu.VMEM((batch * n_kv, hd), F32), pltpu.VMEM((batch * n_kv, hd), F32),
@@ -293,8 +287,8 @@
 
 
 GROUPS = 2
-SUB = 2
-NCOL = 4
+SUB = 4
+NCOL = 2
 
 
 def mlp_kernel(layer, last, x_in, part_ref, norm_in, next_norm_in, wg_hbm, wu_hbm, wd_hbm, *refs):

time: 95.2 us -> 90 us (0.945)
  Pallas kernels: 93.3 us -> 88.2 us
    pallas_call x2, Pallas kernels: 26.5 us -> 23.1 us  [attention_call(): pl.pallas_call(functools.partial(attention_kernel, layer, first, chunk),...]
    pallas_call x2, Pallas kernels: 66.8 us -> 65.1 us  [mlp_call(): pl.pallas_call(functools.partial(mlp_kernel, layer, last), out_shape=full...]
where the time goes in v7:
time: 90 us; the launch traced here: 89.9 us
  Pallas kernels  88.2 us (98%)
  local copies, waits for them, and re-layouts  0.99 us (1%)
    pallas_call x2, Pallas kernels, mlp_call(): pl.pallas_call(functools.partial(mlp_kernel, layer, last), out_shape=full...  65.1 us
    pallas_call x2, Pallas kernels, attention_call(): pl.pallas_call(functools.partial(attention_kernel, layer, first, chunk),...  23.1 us

profile of v7, /device:TPU:0, one launch (start us, length us, event | category | flops | bytes accessed | tf_op | source)
XLA Modules:
  0.0 89.9 jit_solution(1661752253807251397)
XLA Ops:
  0.6 14.5 %attention0.1 = (bf16[256,2048]{1,0:T(8,128)(2,1)S(1)}, bf16[2,256,128,128]{3,2,1,0:T(8,128)(2,1)}, bf16[2,256,128,128]{3,2,1,0:T(8,128)(2,1)}) custom-call(s32[256]{0:T(256)} %refs_0_.5, bf16[256,2048]{1,0:T(8,128)(2,1)} %x_in.1, bf16[2,2048]{1,0:T(2,128)(2,1)} %next_norm_in.3, f32[64,128]{1,0:T(8,128)} %constant.4.clone.refs_3_.refs_2_, ...), custom_call_target="tpu_custom_call" | custom-call | tf_op jit(solution)/shard_map/attention0/pallas_call | solution.py:277
  15.1 0.0 copy-start
  15.1 0.0 copy-start.1
  15.2 0.0 copy-start.2
  15.2 34.0 %mlp0.1 = (bf16[256,2048]{1,0:T(8,128)(2,1)S(1)}, bf16[128,2048]{1,0:T(8,128)(2,1)S(1)}, bf16[2048,512]{1,0:T(8,128)(2,1)S(1)}, bf16[2048,256]{1,0:T(8,128)(2,1)...) custom-call(bf16[256,2048]{1,0:T(8,128)(2,1)} %x_in.1, ...), custom_call_target="tpu_custom_call" | custom-call | tf_op jit(solution)/shard_map/mlp0/pallas_call | solution.py:504
  49.2 0.0 copy-done
  49.2 0.0 copy-done.1
  49.2 0.0 copy-done.2
  49.2 8.6 %attention1.1 = (bf16[256,2048]{1,0:T(8,128)(2,1)S(1)}, bf16[2,256,128,128]{3,2,1,0:T(8,128)(2,1)}, bf16[2,256,128,128]{3,2,1,0:T(8,128)(2,1)}, bf16[256,128,128...) custom-call(s32[256]{0:T(256)S(1)} %copy-done.2, ...), custom_call_target="tpu_custom_call", output_to_operand_aliasing={{1}: (10, {}), {2}: (11, {}), {3}: (8, {}), {4}: (9, {})} | custom-call | tf_op jit(solution)/shard_map/attention1/pallas_call | solution.py:277
  57.8 31.1 %mlp1.1 = bf16[256,2048]{1,0:T(8,128)(2,1)S(1)} custom-call(bf16[128,2048]{1,0:T(8,128)(2,1)S(1)} %get-tuple-element.18.x_in, bf16[256,2048]{1,0:T(8,128)(2,1)S(1)} %get-tuple-element.28.part_ref, bf16[2,2048]{1,0:T(2,128)(2,1)} %norm_in.3, bf16[2,2048]{1,0:T(2,128)(2,1)} %next_norm_in.3, bf16[2,2048,2048]{2,1,0:T(8,128)(2,1)} %wg_hbm.3, ...), custom_call_target="tpu_custom_call" | custom-call | tf_op jit(solution)/shard_map/mlp1/pallas_call | solution.py:504
  88.9 1.0 %copy.27 = bf16[256,2048]{1,0:T(8,128)(2,1)} copy(bf16[256,2048]{1,0:T(8,128)(2,1)S(1)} %mlp1.1) | data formatting | bytes 2097152
Async XLA Ops:
  15.1 34.0 %copy-start = (f32[64,128]{1,0:T(8,128)S(1)}, f32[64,128]{1,0:T(8,128)}, u32[]{:S(2)}) copy-start(f32[64,128]{1,0:T(8,128)} %constant.5.clone.refs_4_.refs_3_) | copy-start | bytes 98308
  15.1 34.0 %copy-start.1 = (f32[64,128]{1,0:T(8,128)S(1)}, f32[64,128]{1,0:T(8,128)}, u32[]{:S(2)}) copy-start(f32[64,128]{1,0:T(8,128)} %constant.4.clone.refs_3_.refs_2_) | copy-start | bytes 98308
  15.2 34.0 %copy-start.2 = (s32[256]{0:T(256)S(1)}, s32[256]{0:T(256)}, u32[]{:S(2)}) copy-start(s32[256]{0:T(256)} %refs_0_.5) | copy-start | bytes 3076

commit v8 on v7

--- a/solution.py
+++ b/solution.py
@@ -181,19 +181,7 @@
         stores.append((pltpu.make_async_copy(kbuf.at[rows], ko_hbm.at[layer, rows], out_sem.at[0, c]),
                        pltpu.make_async_copy(vbuf.at[rows], vo_hbm.at[layer, rows], out_sem.at[1, c])))
 
-    def values(c):
-        for t in range(quads):
-            b = c * chunk + t * 4
-            p4 = p_scr[c % 2, pl.ds(t * 2 * pair, 2 * pair), :]
-            wide = jnp.concatenate([jnp.where(first_in_pair, p4, zero), jnp.where(first_in_pair, zero, p4)], axis=1).astype(BF16)
-            o = jnp.dot(wide, square(vmat, b * rows_kv), preferred_element_type=F32)
-            o_scr[pl.ds(b * n_q, 2 * pair), :] = jnp.where(first_pair, o[:, :128], o[:, 128:])
-
-    for c in range(n_chunks):
-        if first:
-            kv_loads[c][0].wait()
-            kv_loads[c][1].wait()
-
+    def insert(c):
         for i in range(c * chunk, (c + 1) * chunk, 8):
             writes = []
             for b in range(i, i + 8):
@@ -209,6 +197,25 @@
             for buf, b, block, value in writes:
                 buf[b, block, :] = value
 
+    def values(c):
+        for t in range(quads):
+            b = c * chunk + t * 4
+            p4 = p_scr[c % 2, pl.ds(t * 2 * pair, 2 * pair), :]
+            wide = jnp.concatenate([jnp.where(first_in_pair, p4, zero), jnp.where(first_in_pair, zero, p4)], axis=1).astype(BF16)
+            o = jnp.dot(wide, square(vmat, b * rows_kv), preferred_element_type=F32)
+            o_scr[pl.ds(b * n_q, 2 * pair), :] = jnp.where(first_pair, o[:, :128], o[:, 128:])
+
+    for c in range(n_chunks):
+        if first:
+            kv_loads[c][0].wait()
+            kv_loads[c][1].wait()
+
+        if first:
+            insert(c)
+        elif c == 0:
+            for other in range(n_chunks):
+                insert(other)
+
         q_t = q_scr[pl.ds(c * cols, cols), :].T
         acc = None
         for t in range(quads):
@@ -223,8 +230,10 @@
             acc = d if acc is None else acc + d
         if c > 0:
             values(c - 1)
-        stores[c][0].start()
-        stores[c][1].start()
+        for ready in ([c] if first or c > 1 else [2 * c, 2 * c + 1] if c < 2 else []):
+            if first or c < 2:
+                stores[ready][0].start()
+                stores[ready][1].start()
         s = jnp.where(first_of_two, acc[:rows_kv], acc[rows_kv:])
         limit = jnp.concatenate([lim_scr[pl.ds(c * (cols // 128) + j, 1), :] for j in range(cols // 128)], axis=1)
         s = jnp.where(same_head & (row <= limit), s * scale, -jnp.inf)

time: 90 us -> 90.4 us (level)
  no operation moved by 1% of the time
where the time goes in v8:
time: 90.4 us; the launch traced here: 90.3 us
  Pallas kernels  88.6 us (98%)
  local copies, waits for them, and re-layouts  0.99 us (1%)
    pallas_call x2, Pallas kernels, mlp_call(): pl.pallas_call(functools.partial(mlp_kernel, layer, last), out_shape=full...  65.1 us
    pallas_call x2, Pallas kernels, attention_call(): pl.pallas_call(functools.partial(attention_kernel, layer, first, chunk),...  23.5 us

profile of v8, /device:TPU:0, one launch (start us, length us, event | category | flops | bytes accessed | tf_op | source)
XLA Modules:
  0.0 90.3 jit_solution(18090108642606878287)
XLA Ops:
  0.6 14.5 %attention0.1 = (bf16[256,2048]{1,0:T(8,128)(2,1)S(1)}, bf16[2,256,128,128]{3,2,1,0:T(8,128)(2,1)}, bf16[2,256,128,128]{3,2,1,0:T(8,128)(2,1)}) custom-call(s32[256]{0:T(256)} %refs_0_.5, bf16[256,2048]{1,0:T(8,128)(2,1)} %x_in.1, bf16[2,2048]{1,0:T(2,128)(2,1)} %next_norm_in.3, f32[64,128]{1,0:T(8,128)} %constant.4.clone.refs_3_.refs_2_, ...), custom_call_target="tpu_custom_call" | custom-call | tf_op jit(solution)/shard_map/attention0/pallas_call | solution.py:286
  15.1 0.0 copy-start
  15.1 0.0 copy-start.1
  15.2 0.0 copy-start.2
  15.2 34.0 %mlp0.1 = (bf16[256,2048]{1,0:T(8,128)(2,1)S(1)}, bf16[128,2048]{1,0:T(8,128)(2,1)S(1)}, bf16[2048,512]{1,0:T(8,128)(2,1)S(1)}, bf16[2048,256]{1,0:T(8,128)(2,1)...) custom-call(bf16[256,2048]{1,0:T(8,128)(2,1)} %x_in.1, ...), custom_call_target="tpu_custom_call" | custom-call | tf_op jit(solution)/shard_map/mlp0/pallas_call | solution.py:513
  49.2 0.0 copy-done
  49.2 0.0 copy-done.1
  49.2 0.0 copy-done.2
  49.2 9.0 %attention1.1 = (bf16[256,2048]{1,0:T(8,128)(2,1)S(1)}, bf16[2,256,128,128]{3,2,1,0:T(8,128)(2,1)}, bf16[2,256,128,128]{3,2,1,0:T(8,128)(2,1)}, bf16[256,128,128...) custom-call(s32[256]{0:T(256)S(1)} %copy-done.2, ...), custom_call_target="tpu_custom_call", output_to_operand_aliasing={{1}: (10, {}), {2}: (11, {}), {3}: (8, {}), {4}: (9, {})} | custom-call | tf_op jit(solution)/shard_map/attention1/pallas_call | solution.py:286
  58.2 31.1 %mlp1.1 = bf16[256,2048]{1,0:T(8,128)(2,1)S(1)} custom-call(bf16[128,2048]{1,0:T(8,128)(2,1)S(1)} %get-tuple-element.18.x_in, bf16[256,2048]{1,0:T(8,128)(2,1)S(1)} %get-tuple-element.28.part_ref, bf16[2,2048]{1,0:T(2,128)(2,1)} %norm_in.3, bf16[2,2048]{1,0:T(2,128)(2,1)} %next_norm_in.3, bf16[2,2048,2048]{2,1,0:T(8,128)(2,1)} %wg_hbm.3, ...), custom_call_target="tpu_custom_call" | custom-call | tf_op jit(solution)/shard_map/mlp1/pallas_call | solution.py:513
  89.3 1.0 %copy.27 = bf16[256,2048]{1,0:T(8,128)(2,1)} copy(bf16[256,2048]{1,0:T(8,128)(2,1)S(1)} %mlp1.1) | data formatting | bytes 2097152
Async XLA Ops:
  15.1 34.0 %copy-start = (f32[64,128]{1,0:T(8,128)S(1)}, f32[64,128]{1,0:T(8,128)}, u32[]{:S(2)}) copy-start(f32[64,128]{1,0:T(8,128)} %constant.5.clone.refs_4_.refs_3_) | copy-start | bytes 98308
  15.1 34.0 %copy-start.1 = (f32[64,128]{1,0:T(8,128)S(1)}, f32[64,128]{1,0:T(8,128)}, u32[]{:S(2)}) copy-start(f32[64,128]{1,0:T(8,128)} %constant.4.clone.refs_3_.refs_2_) | copy-start | bytes 98308
  15.2 34.0 %copy-start.2 = (s32[256]{0:T(256)S(1)}, s32[256]{0:T(256)}, u32[]{:S(2)}) copy-start(s32[256]{0:T(256)} %refs_0_.5) | copy-start | bytes 3076
